TPU v7x, 128 devices: a whole 4x4x4 slice. The times are simulated.
128 devices in a mesh: don: 8 (over x, core), acc: 16 (over y, z).
Axes of the slice: x: 4, y: 4, z: 4, core: 2. Of those that a mesh axis runs over, the one named last changes fastest.
Arguments:
- donor_emb: bfloat16 [262144, 768], P(('don', 'acc')), may hold values from -12 to 12
- acceptor_emb: bfloat16 [262144, 768], P(('don', 'acc')), may hold values from -6 to 6
- donor_pos: int32 [3072], P(('don', 'acc')), may hold values from 0 to 2047
- acceptor_pos: int32 [3072], P(('don', 'acc')), may hold values from 0 to 2047
- donor_count: int32 [128], P('don'), may hold values from 1 to 24, as said below
- acceptor_count: int32 [128], replicated, may hold values from 1 to 24, as said below
- target: int32 [64, 3072], P(None, 'don'), may hold values from 0 to 3071, as said below
- junction_mask: int32 [64, 3072], P(None, 'don'), may hold values 0 or 1
- weights: bfloat16 [64, 768, 768], P('acc'), may hold values from -1 to 2
Outputs:
- loss: float32 [], replicated
- grad_weight: float32 [768, 64, 768], P('don', 'acc')
Inputs may be any that keep to these rules, and one draw needn't show every extreme that they name: `donor_count`: the live donor slots of all shards number exactly 1600; some shard has all 24 live. `acceptor_count`: the live acceptor slots of all shards number exactly 1600; some shard has all 24 live. `target`: each entry names a live acceptor slot.
All inputs are finite; a program needn't handle non-finite values. No bound on the sum of `junction_mask` on one device may be relied on, other than what follows from the above.
Results may differ from a plain program's by a relative error of at most 0.0031.
Values may be sent and summed in bfloat16 or wider, within the bound.
No kernel may reach another device: no remote copies, remote signals or barrier semaphores. Data moves between devices by JAX's collectives and lax.ppermute only.
A program may use at most 128 MiB of HBM per device.

v0:
```python
import itertools

import jax
import jax.numpy as jnp
from jax import lax
from jax.experimental import pallas as pl
from jax.experimental.pallas import tpu as pltpu
from jax.sharding import Mesh
from jax.sharding import PartitionSpec as P


AXES = ("x", "c", "y", "z")
SIZES = (4, 2, 4, 4)
CAP = 24
LIVE = 1600
COLS = 1664
ROWS_A = 1744
MAIN = 1536
MB = 256
PIECE = 16 * CAP
SUB = 128
F32 = jnp.float32
BF16 = jnp.bfloat16
I32 = jnp.int32


def exchange_pairs(axis_core0, axis_core1, mask):
    pairs = []
    for coords in itertools.product(*(range(n) for n in SIZES)):
        moved = list(coords)
        axis = AXES.index(axis_core1 if coords[1] else axis_core0)
        moved[axis] ^= mask
        source = target = 0
        for n, a, b in zip(SIZES, coords, moved):
            source, target = source * n + a, target * n + b
        pairs.append((source, target))
    return pairs


def exchange(value, axis_core0, axis_core1, mask):
    return lax.ppermute(value, AXES, exchange_pairs(axis_core0, axis_core1, mask))


def swap_core(value):
    return lax.ppermute(value, "c", [(0, 1), (1, 0)])


def site_kernel(
    apos_ref,
    dpos_ref,
    count_ref,
    aemb_ref,
    demb_ref,
    target_ref,
    mask_ref,
    out_ref,
    rows_ref,
    picked_ref,
    sems,
):
    sites = 2 * CAP
    copies = []
    picks = lax.broadcasted_iota(I32, (sites, 8 * sites), 0)
    lanes = lax.broadcasted_iota(I32, (sites, 8 * sites), 1)
    column = lax.axis_index("y") * 4 + lax.axis_index("z")
    tissues = pl.multiple_of((column // 2) * 8, 8)
    for i, ref in enumerate((target_ref, mask_ref)):
        copies.append(
            pltpu.make_async_copy(
                ref.at[pl.ds(tissues, 8), :], picked_ref.at[i], sems.at[sites + i]
            )
        )
        copies[-1].start()
    wanted = picks * 8
    for i in range(sites):
        emb_ref, pos = (aemb_ref, apos_ref[i]) if i < CAP else (demb_ref, dpos_ref[i - CAP])
        group = pl.multiple_of((pos // 8) * 8, 8)
        copies.append(
            pltpu.make_async_copy(
                emb_ref.at[pl.ds(group, 8), :], rows_ref.at[pl.ds(8 * i, 8), :], sems.at[i]
            )
        )
        copies[-1].start()
        wanted = jnp.where(picks == i, wanted + (pos - group), wanted)
    onehot = jnp.where(lanes == wanted, 1.0, 0.0).astype(BF16)

    lane = lax.broadcasted_iota(I32, (4, PIECE), 1)
    shard = (lane * 2731) >> 16
    limit = jnp.zeros((4, PIECE), I32)
    for i in range(16):
        limit = jnp.where(shard == i, count_ref[i], limit)
    live = lane - shard * CAP < limit
    for copy in copies[:2]:
        copy.wait()
    upper = column % 2 == 1
    targets = jnp.where(upper, picked_ref[0, 4:8, :], picked_ref[0, 0:4, :])
    masks = jnp.where(upper, picked_ref[1, 4:8, :], picked_ref[1, 0:4, :])
    value = jnp.where(live & (masks > 0), targets, -1)
    halves = jnp.concatenate([value >> 6, value & 63], axis=1).astype(F32)
    halves = jnp.concatenate([halves, jnp.zeros_like(halves)], axis=0)
    out_ref[sites : sites + 8, :] = halves.astype(BF16)

    for copy in copies[2:]:
        copy.wait()
    out_ref[0:sites, :] = jnp.dot(
        onehot, rows_ref[...], preferred_element_type=F32
    ).astype(BF16)


def output_kernel(own_ref, one_ref, two_ref, three_ref, out_ref):
    x = lax.axis_index("x")
    for m, ref in enumerate((own_ref, one_ref, two_ref, three_ref)):
        out_ref[:, pl.ds(x ^ m, 1), :] = ref[...].astype(F32)[:, None, :]


def one_hot(hit):
    return jnp.where(hit, 1.0, 0.0).astype(BF16)


def as_rows(row):
    return jnp.broadcast_to(row, (8, SUB)).astype(BF16)


def acceptor_tables(count_row, x, c, y, z):
    lane = lax.broadcasted_iota(I32, (1, SUB), 1)
    sub = lax.broadcasted_iota(I32, (SUB, SUB), 0)
    m3, m2, m1 = (lane >> 4) & 3, (lane >> 2) & 3, lane & 3
    core = c ^ (lane >> 6)
    shard0 = (x ^ m3) * 32 + (y ^ m1) * 4 + (z ^ m2)
    shard1 = (x ^ m2) * 32 + 16 + (y ^ m3) * 4 + (z ^ m1)
    shard = jnp.where(core == 0, shard0, shard1)
    counts = jnp.dot(
        as_rows(count_row.astype(F32)), one_hot(sub == shard), preferred_element_type=F32
    )
    offsets = jnp.dot(
        counts.astype(BF16), one_hot(sub < lane), preferred_element_type=F32
    ).astype(I32)
    counts_row = counts.astype(I32)[0:1, :]
    row = lax.broadcasted_iota(I32, (8, SUB), 0)
    table = jnp.where(row == 0, counts.astype(I32), jnp.where(row == 1, offsets >> 6, offsets & 63))
    table = table.astype(F32).astype(BF16)
    ranks, starts = [], []
    for b in range(8 * PIECE // SUB):
        slot = b * SUB + lane
        place = (slot * 2731) >> 16
        within = slot - place * CAP
        here = jnp.dot(table, one_hot(sub == place), preferred_element_type=F32).astype(I32)
        rank = here[1:2, :] * 64 + here[2:3, :] + within
        ranks.append(jnp.where(within < here[0:1, :], rank, -1))
        before = jnp.minimum(jnp.maximum(b * SUB - CAP * lane, 0), counts_row)
        starts.append(jnp.sum(before.astype(F32)).astype(I32))
    return offsets[0:1, :], ranks, starts


def donor_tables(rows, x, c, y, z):
    lane = lax.broadcasted_iota(I32, (1, SUB), 1)
    sub = lax.broadcasted_iota(I32, (SUB, SUB), 0)
    row = lax.broadcasted_iota(I32, (8, SUB), 0)
    pick = lax.broadcasted_iota(I32, (8, 2 * PIECE), 0) == x
    lines = [
        jnp.sum(jnp.where(pick, r.astype(F32), 0.0), axis=0, keepdims=True) for r in rows
    ]
    sources = []
    for u in range(PIECE // SUB):
        low, high = u * SUB, (u + 1) * SUB
        stack = [line[:, low:high] for line in lines]
        stack += [line[:, PIECE + low : PIECE + high] for line in lines]
        sources.append(jnp.concatenate(stack, axis=0).astype(BF16))
    values = []
    for m3 in range(4):
        for v in range(PIECE // SUB):
            slot = v * SUB + lane
            place = (slot * 2731) >> 16
            within = slot - place * CAP
            m2, m1 = place >> 2, place & 3
            natural0 = (y ^ m1) * 4 + (z ^ m2)
            natural1 = (y ^ m3) * 4 + (z ^ m1)
            natural = jnp.where(c == 0, natural0, natural1) * CAP + within
            wanted = jnp.where(c == 0, m3, m2)
            moved = sum(
                jnp.dot(source, one_hot(sub + u * SUB == natural), preferred_element_type=F32)
                for u, source in enumerate(sources)
            )
            moved = jnp.where((row & 3) == wanted, moved, 0.0)
            moved = moved * jnp.where(row < 4, 64.0, 1.0)
            values.append(jnp.sum(moved, axis=0, keepdims=True).astype(I32))
    return values


def compact(dst_ref, source, rank_row, start):
    base = pl.multiple_of((start // 16) * 16, 16)
    hit = lax.broadcasted_iota(I32, (SUB + 16, SUB), 0) == rank_row - base
    picked = jnp.dot(
        jnp.where(hit, 1.0, 0.0).astype(BF16), source, preferred_element_type=F32
    ).astype(BF16)
    dst_ref[pl.ds(base, 16), :] = dst_ref[pl.ds(base, 16), :] + picked[:16]
    dst_ref[pl.ds(base + 16, SUB), :] = picked[16:]
    return hit, base


def acceptor_kernel(count_ref, lines_ref, *refs):
    pieces = refs[:8]
    acc_ref, offset_ref, value_ref, rank_ref, starts_ref = refs[8:]
    width = acc_ref.shape[1]
    x, c, y, z = (lax.axis_index(a) for a in AXES)
    blocks = PIECE // SUB

    rows = [
        jnp.where(c == 0, pieces[i][PIECE : PIECE + 8, :], lines_ref[i]) for i in range(4)
    ]
    lower = lax.broadcasted_iota(I32, (SUB, SUB), 0) <= lax.broadcasted_iota(I32, (SUB, SUB), 1)
    lower = one_hot(lower)
    count = 0
    for b, row in enumerate(donor_tables(rows, x, c, y, z)):
        starts_ref[b] = count
        active = jnp.where(row >= 0, 1.0, 0.0)
        inclusive = jnp.dot(as_rows(active), lower, preferred_element_type=F32).astype(I32)
        rank_ref[b : b + 1, :] = jnp.where(row >= 0, inclusive[0:1, :] - 1 + count, -1)
        value_ref[b : b + 1, :] = row
        count = count + jnp.sum(active).astype(I32)
    starts_ref[4 * blocks] = count

    offset_row, ranks, starts_a = acceptor_tables(count_ref[...], x, c, y, z)
    offset_ref[...] = jnp.broadcast_to(offset_row, (8, SUB))
    acc_ref[0:16, :] = jnp.zeros((16, width), BF16)
    for b in range(8 * blocks):
        i, j = b // blocks, b % blocks
        compact(acc_ref, pieces[i][j * SUB : (j + 1) * SUB, :], ranks[b], starts_a[b])
    acc_ref[LIVE:COLS, :] = jnp.zeros((COLS - LIVE, width), BF16)


def head_kernel(starts_ref, acc_ref, offset_ref, value_ref, rank_ref, w_ref, *refs):
    pieces = refs[:4]
    keep_ref, send_ref, sums_ref = refs[4:7]
    rows_ref, tval_ref, grad_ref, num_ref = refs[7:]
    width = w_ref.shape[0]
    scale = width ** (-0.5)
    x, c, y, z = (lax.axis_index(a) for a in AXES)
    blocks = PIECE // SUB
    count = starts_ref[4 * blocks]
    offset_row = offset_ref[0:1, :]

    rows_ref[0:16, :] = jnp.zeros((16, width), BF16)
    tval_ref[0:16, :] = jnp.zeros((16, SUB), I32)
    grad_ref[...] = jnp.zeros((width, width), F32)
    num_ref[...] = jnp.zeros((8, SUB), F32)
    for b in range(4 * blocks):
        i, j = b // blocks, b % blocks
        source = pieces[i][j * SUB : (j + 1) * SUB, :]
        hit, base = compact(rows_ref, source, rank_ref[b : b + 1, :], starts_ref[b])
        chosen = jnp.sum(jnp.where(hit, value_ref[b : b + 1, :], 0), axis=1, keepdims=True)
        chosen = jnp.broadcast_to(chosen, (SUB + 16, SUB))
        tval_ref[pl.ds(base, 16), :] = tval_ref[pl.ds(base, 16), :] + chosen[:16]
        tval_ref[pl.ds(base + 16, SUB), :] = chosen[16:]
    tail = pl.multiple_of(((count + 15) // 16) * 16, 16)
    rows_ref[pl.ds(tail, MB), :] = jnp.zeros((MB, width), BF16)
    tval_ref[pl.ds(tail, MB), :] = jnp.zeros((MB, SUB), I32)

    def block(i, carry):
        first = pl.multiple_of(i * MB, MB)
        donors = rows_ref[pl.ds(first, MB), :]
        slot = tval_ref[pl.ds(first, MB), :]
        shard = (slot * 2731) >> 16
        within = slot - shard * CAP
        mx = (shard >> 5) ^ x
        core = (shard >> 4) & 1
        my = ((shard >> 2) & 3) ^ y
        mz = (shard & 3) ^ z
        place = jnp.where(core == 0, mx * 16 + mz * 4 + my, my * 16 + mx * 4 + mz)
        place = place + jnp.where(core == c, 0, 64)
        found = place == lax.broadcasted_iota(I32, (MB, SUB), 1)
        column = jnp.sum(jnp.where(found, offset_row + within, 0), axis=1, keepdims=True)

        projected = jnp.dot(donors, w_ref[...], preferred_element_type=F32).astype(BF16)
        groups = ((0, MAIN), (MAIN, COLS))
        scores, targets = [], []
        for low, high in groups:
            part = lax.dot_general(
                projected,
                acc_ref[low:high, :],
                (((1,), (1,)), ((), ())),
                preferred_element_type=F32,
            )
            columns = low + lax.broadcasted_iota(I32, (MB, high - low), 1)
            part = part * scale
            if high > LIVE:
                part = jnp.where(columns < LIVE, part, -1e30)
            scores.append(part)
            targets.append(columns == column)
        highest = jnp.maximum(*(jnp.max(part, axis=1, keepdims=True) for part in scores))
        exped = [jnp.exp(part - highest) for part in scores]
        exped[1] = jnp.where(scores[1] > -1e29, exped[1], 0.0)
        summed = sum(jnp.sum(part, axis=1, keepdims=True) for part in exped)
        picked = sum(
            jnp.sum(jnp.where(hit, part, 0.0), axis=1, keepdims=True)
            for hit, part in zip(targets, scores)
        )
        here = first + lax.broadcasted_iota(I32, (MB, 1), 0) < count
        loss = jnp.where(here, highest + jnp.log(summed) - picked, 0.0)
        num_ref[0:1, :] = num_ref[0:1, :] + jnp.sum(loss)
        inverse = jnp.where(here, 1.0 / summed, 0.0)
        minus = jnp.where(here, 1.0, 0.0)
        dproj = 0.0
        for (low, high), part, hit in zip(groups, exped, targets):
            dscore = (part * inverse - jnp.where(hit, minus, 0.0)).astype(BF16)
            dproj = dproj + jnp.dot(dscore, acc_ref[low:high, :], preferred_element_type=F32)
        dproj = (dproj * scale).astype(BF16)
        grad_ref[...] += lax.dot_general(
            donors, dproj, (((0,), (0,)), ((), ())), preferred_element_type=F32
        )
        return carry

    lax.fori_loop(0, (count + MB - 1) // MB, block, 0)

    lanes = lax.broadcasted_iota(I32, (8, SUB), 1)
    sums_ref[...] = jnp.where(lanes == 0, num_ref[0:1, :], count.astype(F32))
    part = width // 8
    for m in range(4):
        keep = pl.multiple_of((2 * (x ^ m) + c) * part, 8)
        send = pl.multiple_of((2 * (x ^ m) + 1 - c) * part, 8)
        keep_ref[m] = grad_ref[pl.ds(keep, part), :]
        send_ref[m] = grad_ref[pl.ds(send, part), :].astype(BF16)


def combine_kernel(keep_ref, received_ref, sums_ref, other_ref, *out_refs):
    for m in range(4):
        out_refs[m][...] = (keep_ref[m] + received_ref[m].astype(F32)).astype(BF16)
    out_refs[4][...] = sums_ref[...] + other_ref[...]


def spread_kernel(own_ref, one_ref, two_ref, three_ref, out_ref):
    sums = (own_ref[...] + one_ref[...]) + (two_ref[...] + three_ref[...])
    out_ref[...] = jnp.broadcast_to(sums[None], out_ref.shape)


def local(
    donor_emb,
    acceptor_emb,
    donor_pos,
    acceptor_pos,
    donor_count,
    acceptor_count,
    target,
    junction_mask,
    weights,
):
    width = weights.shape[1]
    part = width // 8
    vmem = pl.BlockSpec(memory_space=pltpu.VMEM)
    smem = pl.BlockSpec(memory_space=pltpu.SMEM)
    any_space = pl.BlockSpec(memory_space=pl.ANY)
    sites = 2 * CAP
    block = pl.pallas_call(
        site_kernel,
        out_shape=jax.ShapeDtypeStruct((sites + 8, width), BF16),
        in_specs=[smem] * 3 + [any_space] * 4,
        out_specs=vmem,
        scratch_shapes=[
            pltpu.VMEM((8 * sites, width), BF16),
            pltpu.VMEM((2, 8, PIECE), I32),
            pltpu.SemaphoreType.DMA((sites + 2,)),
        ],
        name="site_rows",
    )(acceptor_pos, donor_pos, donor_count, acceptor_emb, donor_emb, target, junction_mask)
    lines = block[sites:]

    block = jnp.stack([block] + [exchange(block, "y", "z", m) for m in (1, 2, 3)])
    block = jnp.stack([block] + [exchange(block, "z", "x", m) for m in (1, 2, 3)])
    acceptors = jnp.concatenate([block[:, :, :CAP].reshape(PIECE, width), lines])
    donors = block[:, :, CAP:sites].reshape(PIECE, width)
    all_lines = block[:, 0, sites:]
    acceptors = [acceptors] + [exchange(acceptors, "x", "y", m) for m in (1, 2, 3)]
    donors = [donors] + [exchange(donors, "x", "y", m) for m in (1, 2, 3)]
    others = []
    for piece in acceptors:
        others.append(swap_core(piece))

    near = pltpu.MemorySpace.VMEM

    def call(kernel, limit, outs, operands, scratch=(), scalars=(), specs=vmem):
        operands = [pltpu.with_memory_space_constraint(o, near) for o in operands]
        return pl.pallas_call(
            kernel,
            out_shape=outs,
            in_specs=[smem] * len(scalars) + [vmem] * len(operands),
            out_specs=specs,
            scratch_shapes=list(scratch),
            compiler_params=pltpu.CompilerParams(vmem_limit_bytes=limit * 2**20),
        )(*scalars, *operands)

    compacted, offsets, values, ranks, starts = call(
        acceptor_kernel,
        24,
        (
            near((ROWS_A, width), BF16),
            near((8, SUB), I32),
            near((16, SUB), I32),
            near((16, SUB), I32),
            jax.ShapeDtypeStruct((16,), I32),
        ),
        (acceptor_count.reshape(1, 128), all_lines, *acceptors, *others),
        specs=(vmem,) * 4 + (smem,),
    )
    tissue = lax.dynamic_index_in_dim(weights, lax.axis_index("x"), 0, False)
    keep, send, sums = call(
        head_kernel,
        36,
        (
            near((4, part, width), F32),
            near((4, part, width), BF16),
            near((8, SUB), F32),
        ),
        (compacted, offsets, values, ranks, tissue, *donors),
        (
            pltpu.VMEM((4 * PIECE + MB + 16, width), BF16),
            pltpu.VMEM((4 * PIECE + MB + 16, SUB), I32),
            pltpu.VMEM((width, width), F32),
            pltpu.VMEM((8, SUB), F32),
        ),
        (starts,),
        specs=(vmem,) * 3,
    )

    other = swap_core(sums)
    received = swap_core(send)
    *total, sums = call(
        combine_kernel,
        12,
        (near((part, width), BF16),) * 4 + (near((8, SUB), F32),),
        (keep, received, sums, other),
        specs=(vmem,) * 5,
    )
    spread = [total[0]] + [exchange(total[m], "x", "x", m) for m in (1, 2, 3)]
    sums = call(
        spread_kernel,
        12,
        near((16, 8, SUB), F32),
        [sums] + [exchange(sums, "x", "x", m) for m in (1, 2, 3)],
    )
    sums = lax.all_to_all(sums, ("y", "z"), 0, 0, tiled=True)
    sums = jnp.sum(sums[:, 0, :2], axis=0)
    loss = sums[0] / jnp.maximum(sums[1], 1.0)

    grad_weight = call(output_kernel, 12, jax.ShapeDtypeStruct((part, 4, width), F32), spread)
    return (loss, grad_weight)


def solution(mesh):
    finer = Mesh(mesh.devices.reshape(SIZES), AXES)
    don, acc = ("x", "c"), ("y", "z")
    return jax.shard_map(
        local,
        mesh=finer,
        in_specs=(
            P(AXES, None),
            P(AXES, None),
            P(AXES),
            P(AXES),
            P(don),
            P(),
            P(None, don),
            P(None, don),
            P(acc, None, None),
        ),
        out_specs=(P(), P(don, acc, None)),
        check_vma=False,
    )
```

profile of v0, /device:TPU:0, one launch (start us, length us, event | category | flops | bytes accessed | tf_op | source)
XLA Modules:
  0.0 111.2 jit_solution(5100535158369691176)
XLA Ops:
  0.6 3.2 %site_rows.1 = bf16[56,768]{1,0:T(8,128)(2,1)} custom-call(s32[24]{0:T(128)} %apos_ref.1, s32[24]{0:T(128)} %dpos_ref.1, s32[16]{0:T(128)} %count_ref.1, bf16[2048,768]{1,0:T(8,128)(2,1)} %aemb_ref.1, bf16[2048,768]{1,0:T(8,128)(2,1)} %demb_ref.1, s32[64,384]{1,0:T(8,128)} %target_ref.1, s32[64,384]{1,0:T(8,128)} %mask_ref.1), custom_call_target="tpu_custom_call" | custom-call | tf_op jit(solution)/shard_map/site_rows/pallas_call | solution.py:353
  3.8 1.8 %collective-permute-start = (bf16[56,768]{1,0:T(8,128)(2,1)}, bf16[56,768]{1,0:T(8,128)(2,1)S(1)}, u32[]{:S(2)}, u32[]{:S(2)}) collective-permute-start(bf16[56,768]{1,0:T(8,128)(2,1)} %site_rows.1), channel_id=1, source_target_pairs={{0,4},{1,5},{2,6},{3,7},{4,0},{5,1},{6,2},{7,3},{8,12},{9,13},{10,... | collective-permute-start | bytes 258056 | tf_op jit(solution)/shard_map/ppermute | solution.py:41
  5.6 2.9 %collective-permute-start.1 = (bf16[56,768]{1,0:T(8,128)(2,1)}, bf16[56,768]{1,0:T(8,128)(2,1)S(1)}, u32[]{:S(2)}, u32[]{:S(2)}) collective-permute-start(bf16[56,768]{1,0:T(8,128)(2,1)} %site_rows.1), channel_id=1, source_target_pairs={{0,8},{1,9},{2,10},{3,11},{4,12},{5,13},{6,14},{7,15},{8,0},{9,1},... | collective-permute-start | bytes 258056 | tf_op jit(solution)/shard_map/ppermute | solution.py:41
  8.5 0.1 collective-permute-start.2
  8.6 0.0 collective-permute-done
  8.6 3.5 %collective-permute-done.1 = bf16[56,768]{1,0:T(8,128)(2,1)S(1)} collective-permute-done((bf16[56,768]{1,0:T(8,128)(2,1)}, bf16[56,768]{1,0:T(8,128)(2,1)S(1)}, u32[]{:S(2)}, u32[]{:S(2)}) %collective-permute-start.1) | collective-permute-done | bytes 86048 | tf_op jit(solution)/shard_map/ppermute | solution.py:41
  12.1 2.3 %collective-permute-done.2 = bf16[56,768]{1,0:T(8,128)(2,1)S(1)} collective-permute-done((bf16[56,768]{1,0:T(8,128)(2,1)}, bf16[56,768]{1,0:T(8,128)(2,1)S(1)}, u32[]{:S(2)}, u32[]{:S(2)}) %collective-permute-start.2) | collective-permute-done | bytes 86048 | tf_op jit(solution)/shard_map/ppermute | solution.py:41
  14.4 0.9 fusion
  15.4 4.0 %collective-permute-start.4 = (bf16[4,56,768]{2,1,0:T(8,128)(2,1)S(1)}, bf16[4,56,768]{2,1,0:T(8,128)(2,1)S(1)}, u32[]{:S(2)}, u32[]{:S(2)}) collective-permute-start(bf16[4,56,768]{2,1,0:T(8,128)(2,1)S(1)} %get-tuple-element.31), channel_id=1, source_target_pairs={{0,2},{1,3},{2,0},{3,1},{4,6},{5,7},{6,4},{7,5},{8,10},{9,11},{10,... | collective-permute-start | bytes 1032200 | tf_op jit(solution)/shard_map/ppermute | solution.py:41
  19.3 0.7 collective-permute-start.5
  20.0 0.3 collective-permute-start.3
  20.3 0.7 slice.28
  21.0 3.5 %collective-permute-done.4 = bf16[4,56,768]{2,1,0:T(8,128)(2,1)S(1)} collective-permute-done((bf16[4,56,768]{2,1,0:T(8,128)(2,1)S(1)}, bf16[4,56,768]{2,1,0:T(8,128)(2,1)S(1)}, u32[]{:S(2)}, u32[]{:S(2)}) %collective-permute-start.4) | collective-permute-done | bytes 344096 | tf_op jit(solution)/shard_map/ppermute | solution.py:41
  24.6 3.6 %collective-permute-done.5 = bf16[4,56,768]{2,1,0:T(8,128)(2,1)S(1)} collective-permute-done((bf16[4,56,768]{2,1,0:T(8,128)(2,1)S(1)}, bf16[4,56,768]{2,1,0:T(8,128)(2,1)S(1)}, u32[]{:S(2)}, u32[]{:S(2)}) %collective-permute-start.5) | collective-permute-done | bytes 344096 | tf_op jit(solution)/shard_map/ppermute | solution.py:41
  28.2 1.1 collective-permute-done.3
  29.3 0.1 pad_maximum_fusion.1
  29.4 0.6 copy-done.9
  30.1 1.6 %collective-permute-start.6 = (bf16[392,768]{1,0:T(8,128)(2,1)S(1)}, bf16[392,768]{1,0:T(8,128)(2,1)S(1)}, u32[]{:S(2)}, u32[]{:S(2)}) collective-permute-start(bf16[392,768]{1,0:T(8,128)(2,1)S(1)} %pad_maximum_fusion.refs_0_), channel_id=1, source_target_pairs={{0,32},{1,33},{2,34},{3,35},{4,36},{5,37},{6,38},{7,39},{8,40},{9,... | collective-permute-start | bytes 1806344 | tf_op jit(solution)/shard_map/ppermute | solution.py:41
  31.7 2.7 %collective-permute-start.7 = (bf16[392,768]{1,0:T(8,128)(2,1)S(1)}, bf16[392,768]{1,0:T(8,128)(2,1)S(1)}, u32[]{:S(2)}, u32[]{:S(2)}) collective-permute-start(bf16[392,768]{1,0:T(8,128)(2,1)S(1)} %pad_maximum_fusion.refs_0_), channel_id=1, source_target_pairs={{0,64},{1,65},{2,66},{3,67},{4,68},{5,69},{6,70},{7,71},{8,72},{9,... | collective-permute-start | bytes 1806344 | tf_op jit(solution)/shard_map/ppermute | solution.py:41
  34.4 0.5 collective-permute-start.8
  34.9 0.0 collective-permute-start.9
  34.9 5.3 %collective-permute-done.6.refs_1_ = bf16[392,768]{1,0:T(8,128)(2,1)S(1)} collective-permute-done((bf16[392,768]{1,0:T(8,128)(2,1)S(1)}, bf16[392,768]{1,0:T(8,128)(2,1)S(1)}, u32[]{:S(2)}, u32[]{:S(2)}) %collective-permute-start.6) | collective-permute-done | bytes 602144 | tf_op jit(solution)/shard_map/ppermute | solution.py:41
  40.2 0.0 collective-permute-start.10
  40.2 8.7 %collective-permute-done.7.refs_2_ = bf16[392,768]{1,0:T(8,128)(2,1)S(1)} collective-permute-done((bf16[392,768]{1,0:T(8,128)(2,1)S(1)}, bf16[392,768]{1,0:T(8,128)(2,1)S(1)}, u32[]{:S(2)}, u32[]{:S(2)}) %collective-permute-start.7) | collective-permute-done | bytes 602144 | tf_op jit(solution)/shard_map/ppermute | solution.py:41
  48.9 0.0 collective-permute-start.11
  48.9 3.1 %collective-permute-done.8.refs_3_ = bf16[392,768]{1,0:T(8,128)(2,1)S(1)} collective-permute-done((bf16[392,768]{1,0:T(8,128)(2,1)S(1)}, bf16[392,768]{1,0:T(8,128)(2,1)S(1)}, u32[]{:S(2)}, u32[]{:S(2)}) %collective-permute-start.8) | collective-permute-done | bytes 602144 | tf_op jit(solution)/shard_map/ppermute | solution.py:41
  52.1 0.1 collective-permute-start.13
  52.2 0.0 collective-permute-done.9.refs_4_
  52.2 0.0 copy-start
  52.2 0.8 copy-done
  53.1 1.9 %collective-permute-start.14 = (bf16[384,768]{1,0:T(8,128)(2,1)S(1)}, bf16[384,768]{1,0:T(8,128)(2,1)}, u32[]{:S(2)}, u32[]{:S(2)}) collective-permute-start(bf16[384,768]{1,0:T(8,128)(2,1)S(1)} %bitcast.24), channel_id=1, source_target_pairs={{0,64},{1,65},{2,66},{3,67},{4,68},{5,69},{6,70},{7,71},{8,72},{9,... | collective-permute-start | bytes 1769480 | tf_op jit(solution)/shard_map/ppermute | solution.py:41
  55.0 0.0 collective-permute-done.10.refs_5_
  55.0 0.8 copy-done.2
  55.8 2.8 %collective-permute-start.15 = (bf16[384,768]{1,0:T(8,128)(2,1)S(1)}, bf16[384,768]{1,0:T(8,128)(2,1)}, u32[]{:S(2)}, u32[]{:S(2)}) collective-permute-start(bf16[384,768]{1,0:T(8,128)(2,1)S(1)} %bitcast.25), channel_id=1, source_target_pairs={{0,96},{1,97},{2,98},{3,99},{4,100},{5,101},{6,102},{7,103},{8,104... | collective-permute-start | bytes 1769480 | tf_op jit(solution)/shard_map/ppermute | solution.py:41
  58.6 1.4 %dynamic-slice_bitcast_fusion.w_ref = bf16[768,768]{1,0:T(8,128)(2,1)S(1)} fusion(bf16[4,768,768]{2,1,0:T(8,128)(2,1)} %param.17, s32[]{:T(128)S(6)} %select_n.4), kind=kLoop, calls=%fused_computation | loop fusion | bytes 2359300 | tf_op jit(solution)/shard_map/jit(dynamic_index_in_dim)/squeeze | solution.py:404
  60.0 0.1 copy-done.10
  60.1 0.0 collective-permute-done.11.refs_6_
  60.1 0.0 collective-permute-done.12.refs_7_
  60.1 1.0 copy-done.1
  61.2 0.2 copy-done.3
  61.4 4.0 %shard_map.104 = (bf16[1744,768]{1,0:T(8,128)(2,1)S(1)}, s32[8,128]{1,0:T(8,128)S(1)}, s32[16,128]{1,0:T(8,128)S(1)}, s32[16,128]{1,0:T(8,128)S(1)}, s32[16]{0:T(128)S(1)}) custom-call(s32[1,128]{1,0:T(1,128)S(1)} %bitcast.27, bf16[4,8,768]{2,1,0:T(8,128)(2,1)S(1)} %maximum_bitcast_fusion.lines_ref, bf16[392,768]{1,0:T(8,128)(2,1)S(1)} %pad_maximum_fusion.refs_0_, ...), custom_call_target="tpu_custom_call" | custom-call | tf_op jit(solution)/shard_map/pallas_call | solution.py:382
  65.4 3.2 %collective-permute-done.14.refs_2_ = bf16[384,768]{1,0:T(8,128)(2,1)} collective-permute-done((bf16[384,768]{1,0:T(8,128)(2,1)S(1)}, bf16[384,768]{1,0:T(8,128)(2,1)}, u32[]{:S(2)}, u32[]{:S(2)}) %collective-permute-start.14) | collective-permute-done | bytes 589856 | tf_op jit(solution)/shard_map/ppermute | solution.py:41
  68.5 4.8 %collective-permute-done.15.refs_3_ = bf16[384,768]{1,0:T(8,128)(2,1)} collective-permute-done((bf16[384,768]{1,0:T(8,128)(2,1)S(1)}, bf16[384,768]{1,0:T(8,128)(2,1)}, u32[]{:S(2)}, u32[]{:S(2)}) %collective-permute-start.15) | collective-permute-done | bytes 589856 | tf_op jit(solution)/shard_map/ppermute | solution.py:41
  73.3 9.7 %shard_map.105 = (f32[4,96,768]{2,1,0:T(8,128)S(1)}, bf16[4,96,768]{2,1,0:T(8,128)(2,1)S(1)}, f32[8,128]{1,0:T(8,128)S(1)}) custom-call(s32[16]{0:T(128)S(1)} %get-tuple-element.15.starts_ref, bf16[1744,768]{1,0:T(8,128)(2,1)S(1)} %get-tuple-element.16.acc_ref, s32[8,128]{1,0:T(8,128)S(1)} %get-tuple-element.17.offset_ref, ...), custom_call_target="tpu_custom_call" | custom-call | tf_op jit(solution)/shard_map/pallas_call | solution.py:382
  83.0 0.1 collective-permute-start.16
  83.1 0.5 collective-permute-start.17
  83.6 1.5 %collective-permute-done.17.other_ref = f32[8,128]{1,0:T(8,128)S(1)} collective-permute-done((f32[8,128]{1,0:T(8,128)S(1)}, f32[8,128]{1,0:T(8,128)S(1)}, u32[]{:S(2)}, u32[]{:S(2)}) %collective-permute-start.17) | collective-permute-done | bytes 4128 | tf_op jit(solution)/shard_map/ppermute | solution.py:45
  85.1 0.0 collective-permute-done.16.received_ref
  85.1 0.2 shard_map.106
  85.3 0.1 collective-permute-start.18
  85.3 4.2 %collective-permute-start.19 = (f32[8,128]{1,0:T(8,128)S(1)}, f32[8,128]{1,0:T(8,128)S(1)}, u32[]{:S(2)}, u32[]{:S(2)}) collective-permute-start(f32[8,128]{1,0:T(8,128)S(1)} %get-tuple-element.23.own_ref), channel_id=1, source_target_pairs={{0,64},{1,65},{2,66},{3,67},{4,68},{5,69},{6,70},{7,71},{8,72},{9,... | collective-permute-start | bytes 12296 | tf_op jit(solution)/shard_map/ppermute | solution.py:41
  89.5 0.5 collective-permute-start.20
  90.0 0.0 collective-permute-done.18.one_ref
  90.0 1.1 %collective-permute-done.19.two_ref = f32[8,128]{1,0:T(8,128)S(1)} collective-permute-done((f32[8,128]{1,0:T(8,128)S(1)}, f32[8,128]{1,0:T(8,128)S(1)}, u32[]{:S(2)}, u32[]{:S(2)}) %collective-permute-start.19) | collective-permute-done | bytes 4128 | tf_op jit(solution)/shard_map/ppermute | solution.py:41
  91.2 3.2 %collective-permute-done.20.three_ref = f32[8,128]{1,0:T(8,128)S(1)} collective-permute-done((f32[8,128]{1,0:T(8,128)S(1)}, f32[8,128]{1,0:T(8,128)S(1)}, u32[]{:S(2)}, u32[]{:S(2)}) %collective-permute-start.20) | collective-permute-done | bytes 4128 | tf_op jit(solution)/shard_map/ppermute | solution.py:41
  94.4 0.6 shard_map.107
  95.0 4.1 %all-to-all-start = ((f32[16,8,128]{2,1,0:T(8,128)}), f32[16,8,128]{2,1,0:T(8,128)S(1)}, u32[]{:S(2)}, u32[]{:S(2)}) async-start(f32[16,8,128]{2,1,0:T(8,128)} %shard_map.107), calls=%async_computation | async-start | bytes 131072 | tf_op jit(solution)/shard_map/all_to_all | solution.py:440
  99.1 0.1 collective-permute-start.21
  99.2 2.5 %collective-permute-start.22 = (bf16[96,768]{1,0:T(8,128)(2,1)S(1)}, bf16[96,768]{1,0:T(8,128)(2,1)S(1)}, u32[]{:S(2)}, u32[]{:S(2)}) collective-permute-start(bf16[96,768]{1,0:T(8,128)(2,1)S(1)} %get-tuple-element.26), channel_id=1, source_target_pairs={{0,64},{1,65},{2,66},{3,67},{4,68},{5,69},{6,70},{7,71},{8,72},{9,... | collective-permute-start | bytes 442376 | tf_op jit(solution)/shard_map/ppermute | solution.py:41
  101.8 2.1 %collective-permute-start.23 = (bf16[96,768]{1,0:T(8,128)(2,1)S(1)}, bf16[96,768]{1,0:T(8,128)(2,1)S(1)}, u32[]{:S(2)}, u32[]{:S(2)}) collective-permute-start(bf16[96,768]{1,0:T(8,128)(2,1)S(1)} %get-tuple-element.27), channel_id=1, source_target_pairs={{0,96},{1,97},{2,98},{3,99},{4,100},{5,101},{6,102},{7,103},{8,104... | collective-permute-start | bytes 442376 | tf_op jit(solution)/shard_map/ppermute | solution.py:41
  103.9 2.9 %all-to-all-done = f32[16,8,128]{2,1,0:T(8,128)S(1)} async-done(((f32[16,8,128]{2,1,0:T(8,128)}), f32[16,8,128]{2,1,0:T(8,128)S(1)}, u32[]{:S(2)}, u32[]{:S(2)}) %all-to-all-start) | async-done | bytes 65568 | tf_op jit(solution)/shard_map/all_to_all | solution.py:440
  106.8 0.6 fusion.1
  108.7 0.0 collective-permute-done.21.one_ref
  108.8 1.3 %shard_map.108 = f32[96,4,768]{2,1,0:T(4,128)} custom-call(bf16[96,768]{1,0:T(8,128)(2,1)S(1)} %get-tuple-element.24.own_ref, bf16[96,768]{1,0:T(8,128)(2,1)S(1)} %collective-permute-done.21.one_ref, bf16[96,768]{1,0:T(8,128)(2,1)S(1)} %collective-permute-done.22.two_ref, bf16[96,768]{1,0:T(8,128)(2,1)S(1)} %collective-permute-done.23.three_ref), custom_call_target="tpu_custom_call" | custom-call | tf_op jit(solution)/shard_map/pallas_call | solution.py:382
  (24 shorter events, 0.2 us)
Async XLA Ops:
  3.8 4.8 %collective-permute-start = (bf16[56,768]{1,0:T(8,128)(2,1)}, bf16[56,768]{1,0:T(8,128)(2,1)S(1)}, u32[]{:S(2)}, u32[]{:S(2)}) collective-permute-start(bf16[56,768]{1,0:T(8,128)(2,1)} %site_rows.1), channel_id=1, source_target_pairs={{0,4},{1,5},{2,6},{3,7},{4,0},{5,1},{6,2},{7,3},{8,12},{9,13},{10,... | collective-permute-start | bytes 258056 | tf_op jit(solution)/shard_map/ppermute | solution.py:41
  5.6 6.5 %collective-permute-start.1 = (bf16[56,768]{1,0:T(8,128)(2,1)}, bf16[56,768]{1,0:T(8,128)(2,1)S(1)}, u32[]{:S(2)}, u32[]{:S(2)}) collective-permute-start(bf16[56,768]{1,0:T(8,128)(2,1)} %site_rows.1), channel_id=1, source_target_pairs={{0,8},{1,9},{2,10},{3,11},{4,12},{5,13},{6,14},{7,15},{8,0},{9,1},... | collective-permute-start | bytes 258056 | tf_op jit(solution)/shard_map/ppermute | solution.py:41
  8.5 5.9 %collective-permute-start.2 = (bf16[56,768]{1,0:T(8,128)(2,1)}, bf16[56,768]{1,0:T(8,128)(2,1)S(1)}, u32[]{:S(2)}, u32[]{:S(2)}) collective-permute-start(bf16[56,768]{1,0:T(8,128)(2,1)} %site_rows.1), channel_id=1, source_target_pairs={{0,12},{1,13},{2,14},{3,15},{4,8},{5,9},{6,10},{7,11},{8,4},{9,5},... | collective-permute-start | bytes 258056 | tf_op jit(solution)/shard_map/ppermute | solution.py:41
  15.4 9.2 %collective-permute-start.4 = (bf16[4,56,768]{2,1,0:T(8,128)(2,1)S(1)}, bf16[4,56,768]{2,1,0:T(8,128)(2,1)S(1)}, u32[]{:S(2)}, u32[]{:S(2)}) collective-permute-start(bf16[4,56,768]{2,1,0:T(8,128)(2,1)S(1)} %get-tuple-element.31), channel_id=1, source_target_pairs={{0,2},{1,3},{2,0},{3,1},{4,6},{5,7},{6,4},{7,5},{8,10},{9,11},{10,... | collective-permute-start | bytes 1032200 | tf_op jit(solution)/shard_map/ppermute | solution.py:41
  19.3 8.9 %collective-permute-start.5 = (bf16[4,56,768]{2,1,0:T(8,128)(2,1)S(1)}, bf16[4,56,768]{2,1,0:T(8,128)(2,1)S(1)}, u32[]{:S(2)}, u32[]{:S(2)}) collective-permute-start(bf16[4,56,768]{2,1,0:T(8,128)(2,1)S(1)} %get-tuple-element.31), channel_id=1, source_target_pairs={{0,3},{1,2},{2,1},{3,0},{4,7},{5,6},{6,5},{7,4},{8,11},{9,10},{10,... | collective-permute-start | bytes 1032200 | tf_op jit(solution)/shard_map/ppermute | solution.py:41
  20.0 9.3 %collective-permute-start.3 = (bf16[4,56,768]{2,1,0:T(8,128)(2,1)S(1)}, bf16[4,56,768]{2,1,0:T(8,128)(2,1)S(1)}, u32[]{:S(2)}, u32[]{:S(2)}) collective-permute-start(bf16[4,56,768]{2,1,0:T(8,128)(2,1)S(1)} %get-tuple-element.31), channel_id=1, source_target_pairs={{0,1},{1,0},{2,3},{3,2},{4,5},{5,4},{6,7},{7,6},{8,9},{9,8},{10,11... | collective-permute-start | bytes 1032200 | tf_op jit(solution)/shard_map/ppermute | solution.py:41
  24.6 4.8 %copy-start.5 = (bf16[4,56,768]{2,1,0:T(8,128)(2,1)}, bf16[4,56,768]{2,1,0:T(8,128)(2,1)S(1)}, u32[]{:S(2)}) copy-start(bf16[4,56,768]{2,1,0:T(8,128)(2,1)S(1)} %collective-permute-done.4) | copy-start | bytes 1032196
  28.2 1.2 %copy-start.7 = (bf16[4,56,768]{2,1,0:T(8,128)(2,1)}, bf16[4,56,768]{2,1,0:T(8,128)(2,1)S(1)}, u32[]{:S(2)}) copy-start(bf16[4,56,768]{2,1,0:T(8,128)(2,1)S(1)} %collective-permute-done.5) | copy-start | bytes 1032196
  29.3 0.7 copy-start.9
  30.1 10.1 %collective-permute-start.6 = (bf16[392,768]{1,0:T(8,128)(2,1)S(1)}, bf16[392,768]{1,0:T(8,128)(2,1)S(1)}, u32[]{:S(2)}, u32[]{:S(2)}) collective-permute-start(bf16[392,768]{1,0:T(8,128)(2,1)S(1)} %pad_maximum_fusion.refs_0_), channel_id=1, source_target_pairs={{0,32},{1,33},{2,34},{3,35},{4,36},{5,37},{6,38},{7,39},{8,40},{9,... | collective-permute-start | bytes 1806344 | tf_op jit(solution)/shard_map/ppermute | solution.py:41
  31.7 17.3 %collective-permute-start.7 = (bf16[392,768]{1,0:T(8,128)(2,1)S(1)}, bf16[392,768]{1,0:T(8,128)(2,1)S(1)}, u32[]{:S(2)}, u32[]{:S(2)}) collective-permute-start(bf16[392,768]{1,0:T(8,128)(2,1)S(1)} %pad_maximum_fusion.refs_0_), channel_id=1, source_target_pairs={{0,64},{1,65},{2,66},{3,67},{4,68},{5,69},{6,70},{7,71},{8,72},{9,... | collective-permute-start | bytes 1806344 | tf_op jit(solution)/shard_map/ppermute | solution.py:41
  34.4 17.7 %collective-permute-start.8 = (bf16[392,768]{1,0:T(8,128)(2,1)S(1)}, bf16[392,768]{1,0:T(8,128)(2,1)S(1)}, u32[]{:S(2)}, u32[]{:S(2)}) collective-permute-start(bf16[392,768]{1,0:T(8,128)(2,1)S(1)} %pad_maximum_fusion.refs_0_), channel_id=1, source_target_pairs={{0,96},{1,97},{2,98},{3,99},{4,100},{5,101},{6,102},{7,103},{8,104... | collective-permute-start | bytes 1806344 | tf_op jit(solution)/shard_map/ppermute | solution.py:41
  34.9 17.3 %collective-permute-start.9 = (bf16[392,768]{1,0:T(8,128)(2,1)S(1)}, bf16[392,768]{1,0:T(8,128)(2,1)S(1)}, u32[]{:S(2)}, u32[]{:S(2)}) collective-permute-start(bf16[392,768]{1,0:T(8,128)(2,1)S(1)} %pad_maximum_fusion.refs_0_), channel_id=1, source_target_pairs={{0,16},{16,0},{1,17},{17,1},{2,18},{18,2},{3,19},{19,3},{4,20},{20... | collective-permute-start | bytes 1806344 | tf_op jit(solution)/shard_map/ppermute | solution.py:45
  40.2 14.8 %collective-permute-start.10 = (bf16[392,768]{1,0:T(8,128)(2,1)S(1)}, bf16[392,768]{1,0:T(8,128)(2,1)S(1)}, u32[]{:S(2)}, u32[]{:S(2)}) collective-permute-start(bf16[392,768]{1,0:T(8,128)(2,1)S(1)} %collective-permute-done.6.refs_1_), channel_id=1, source_target_pairs={{0,16},{16,0},{1,17},{17,1},{2,18},{18,2},{3,19},{19,3},{4,20},{20... | collective-permute-start | bytes 1806344 | tf_op jit(solution)/shard_map/ppermute | solution.py:45
  48.9 11.2 %collective-permute-start.11 = (bf16[392,768]{1,0:T(8,128)(2,1)S(1)}, bf16[392,768]{1,0:T(8,128)(2,1)}, u32[]{:S(2)}, u32[]{:S(2)}) collective-permute-start(bf16[392,768]{1,0:T(8,128)(2,1)S(1)} %collective-permute-done.7.refs_2_), channel_id=1, source_target_pairs={{0,16},{16,0},{1,17},{17,1},{2,18},{18,2},{3,19},{19,3},{4,20},{20... | collective-permute-start | bytes 1806344 | tf_op jit(solution)/shard_map/ppermute | solution.py:45
  52.1 8.0 %collective-permute-start.12 = (bf16[392,768]{1,0:T(8,128)(2,1)S(1)}, bf16[392,768]{1,0:T(8,128)(2,1)}, u32[]{:S(2)}, u32[]{:S(2)}) collective-permute-start(bf16[392,768]{1,0:T(8,128)(2,1)S(1)} %collective-permute-done.8.refs_3_), channel_id=1, source_target_pairs={{0,16},{16,0},{1,17},{17,1},{2,18},{18,2},{3,19},{19,3},{4,20},{20... | collective-permute-start | bytes 1806344 | tf_op jit(solution)/shard_map/ppermute | solution.py:45
  52.1 13.2 %collective-permute-start.13 = (bf16[384,768]{1,0:T(8,128)(2,1)S(1)}, bf16[384,768]{1,0:T(8,128)(2,1)}, u32[]{:S(2)}, u32[]{:S(2)}) collective-permute-start(bf16[384,768]{1,0:T(8,128)(2,1)S(1)} %bitcast.23), channel_id=1, source_target_pairs={{0,32},{1,33},{2,34},{3,35},{4,36},{5,37},{6,38},{7,39},{8,40},{9,... | collective-permute-start | bytes 1769480 | tf_op jit(solution)/shard_map/ppermute | solution.py:41
  52.2 0.8 copy-start
  53.1 15.5 %collective-permute-start.14 = (bf16[384,768]{1,0:T(8,128)(2,1)S(1)}, bf16[384,768]{1,0:T(8,128)(2,1)}, u32[]{:S(2)}, u32[]{:S(2)}) collective-permute-start(bf16[384,768]{1,0:T(8,128)(2,1)S(1)} %bitcast.24), channel_id=1, source_target_pairs={{0,64},{1,65},{2,66},{3,67},{4,68},{5,69},{6,70},{7,71},{8,72},{9,... | collective-permute-start | bytes 1769480 | tf_op jit(solution)/shard_map/ppermute | solution.py:41
  55.0 0.8 copy-start.2
  55.8 17.5 %collective-permute-start.15 = (bf16[384,768]{1,0:T(8,128)(2,1)S(1)}, bf16[384,768]{1,0:T(8,128)(2,1)}, u32[]{:S(2)}, u32[]{:S(2)}) collective-permute-start(bf16[384,768]{1,0:T(8,128)(2,1)S(1)} %bitcast.25), channel_id=1, source_target_pairs={{0,96},{1,97},{2,98},{3,99},{4,100},{5,101},{6,102},{7,103},{8,104... | collective-permute-start | bytes 1769480 | tf_op jit(solution)/shard_map/ppermute | solution.py:41
  58.6 1.4 %copy-start.6 = (bf16[4,56,768]{2,1,0:T(8,128)(2,1)S(1)}, bf16[4,56,768]{2,1,0:T(8,128)(2,1)}, u32[]{:S(2)}) copy-start(bf16[4,56,768]{2,1,0:T(8,128)(2,1)} %copy-done.5) | copy-start | bytes 1032196
  58.6 1.5 %copy-start.8 = (bf16[4,56,768]{2,1,0:T(8,128)(2,1)S(1)}, bf16[4,56,768]{2,1,0:T(8,128)(2,1)}, u32[]{:S(2)}) copy-start(bf16[4,56,768]{2,1,0:T(8,128)(2,1)} %copy-done.7) | copy-start | bytes 1032196
  58.6 1.5 %copy-start.10 = (bf16[4,56,768]{2,1,0:T(8,128)(2,1)S(1)}, bf16[4,56,768]{2,1,0:T(8,128)(2,1)}, u32[]{:S(2)}) copy-start(bf16[4,56,768]{2,1,0:T(8,128)(2,1)} %copy-done.9) | copy-start | bytes 1032196
  60.1 1.1 copy-start.1
  60.1 1.2 %copy-start.3 = (bf16[392,768]{1,0:T(8,128)(2,1)S(1)}, bf16[392,768]{1,0:T(8,128)(2,1)}, u32[]{:S(2)}) copy-start(bf16[392,768]{1,0:T(8,128)(2,1)} %copy-done.2) | copy-start | bytes 1806340
  60.1 1.2 %copy-start.4 = (s32[128]{0:T(128)S(1)}, s32[128]{0:T(128)}, u32[]{:S(2)}) copy-start(s32[128]{0:T(128)} %param.14) | copy-start | bytes 1540
  83.0 2.1 %collective-permute-start.16 = (bf16[4,96,768]{2,1,0:T(8,128)(2,1)S(1)}, bf16[4,96,768]{2,1,0:T(8,128)(2,1)S(1)}, u32[]{:S(2)}, u32[]{:S(2)}) collective-permute-start(bf16[4,96,768]{2,1,0:T(8,128)(2,1)S(1)} %get-tuple-element.21), channel_id=1, source_target_pairs={{0,16},{16,0},{1,17},{17,1},{2,18},{18,2},{3,19},{19,3},{4,20},{20... | collective-permute-start | bytes 1769480 | tf_op jit(solution)/shard_map/ppermute | solution.py:45
  83.1 2.0 %collective-permute-start.17 = (f32[8,128]{1,0:T(8,128)S(1)}, f32[8,128]{1,0:T(8,128)S(1)}, u32[]{:S(2)}, u32[]{:S(2)}) collective-permute-start(f32[8,128]{1,0:T(8,128)S(1)} %get-tuple-element.22.sums_ref), channel_id=1, source_target_pairs={{0,16},{16,0},{1,17},{17,1},{2,18},{18,2},{3,19},{19,3},{4,20},{20... | collective-permute-start | bytes 12296 | tf_op jit(solution)/shard_map/ppermute | solution.py:45
  85.3 4.8 %collective-permute-start.18 = (f32[8,128]{1,0:T(8,128)S(1)}, f32[8,128]{1,0:T(8,128)S(1)}, u32[]{:S(2)}, u32[]{:S(2)}) collective-permute-start(f32[8,128]{1,0:T(8,128)S(1)} %get-tuple-element.23.own_ref), channel_id=1, source_target_pairs={{0,32},{1,33},{2,34},{3,35},{4,36},{5,37},{6,38},{7,39},{8,40},{9,... | collective-permute-start | bytes 12296 | tf_op jit(solution)/shard_map/ppermute | solution.py:41
  85.3 5.8 %collective-permute-start.19 = (f32[8,128]{1,0:T(8,128)S(1)}, f32[8,128]{1,0:T(8,128)S(1)}, u32[]{:S(2)}, u32[]{:S(2)}) collective-permute-start(f32[8,128]{1,0:T(8,128)S(1)} %get-tuple-element.23.own_ref), channel_id=1, source_target_pairs={{0,64},{1,65},{2,66},{3,67},{4,68},{5,69},{6,70},{7,71},{8,72},{9,... | collective-permute-start | bytes 12296 | tf_op jit(solution)/shard_map/ppermute | solution.py:41
  89.5 4.8 %collective-permute-start.20 = (f32[8,128]{1,0:T(8,128)S(1)}, f32[8,128]{1,0:T(8,128)S(1)}, u32[]{:S(2)}, u32[]{:S(2)}) collective-permute-start(f32[8,128]{1,0:T(8,128)S(1)} %get-tuple-element.23.own_ref), channel_id=1, source_target_pairs={{0,96},{1,97},{2,98},{3,99},{4,100},{5,101},{6,102},{7,103},{8,104... | collective-permute-start | bytes 12296 | tf_op jit(solution)/shard_map/ppermute | solution.py:41
  95.0 11.8 %all-to-all-start = ((f32[16,8,128]{2,1,0:T(8,128)}), f32[16,8,128]{2,1,0:T(8,128)S(1)}, u32[]{:S(2)}, u32[]{:S(2)}) async-start(f32[16,8,128]{2,1,0:T(8,128)} %shard_map.107), calls=%async_computation | async-start | bytes 131072 | tf_op jit(solution)/shard_map/all_to_all | solution.py:440
  99.1 9.6 %collective-permute-start.21 = (bf16[96,768]{1,0:T(8,128)(2,1)S(1)}, bf16[96,768]{1,0:T(8,128)(2,1)S(1)}, u32[]{:S(2)}, u32[]{:S(2)}) collective-permute-start(bf16[96,768]{1,0:T(8,128)(2,1)S(1)} %get-tuple-element.25), channel_id=1, source_target_pairs={{0,32},{1,33},{2,34},{3,35},{4,36},{5,37},{6,38},{7,39},{8,40},{9,... | collective-permute-start | bytes 442376 | tf_op jit(solution)/shard_map/ppermute | solution.py:41
  99.2 9.5 %collective-permute-start.22 = (bf16[96,768]{1,0:T(8,128)(2,1)S(1)}, bf16[96,768]{1,0:T(8,128)(2,1)S(1)}, u32[]{:S(2)}, u32[]{:S(2)}) collective-permute-start(bf16[96,768]{1,0:T(8,128)(2,1)S(1)} %get-tuple-element.26), channel_id=1, source_target_pairs={{0,64},{1,65},{2,66},{3,67},{4,68},{5,69},{6,70},{7,71},{8,72},{9,... | collective-permute-start | bytes 442376 | tf_op jit(solution)/shard_map/ppermute | solution.py:41
  101.8 7.0 %collective-permute-start.23 = (bf16[96,768]{1,0:T(8,128)(2,1)S(1)}, bf16[96,768]{1,0:T(8,128)(2,1)S(1)}, u32[]{:S(2)}, u32[]{:S(2)}) collective-permute-start(bf16[96,768]{1,0:T(8,128)(2,1)S(1)} %get-tuple-element.27), channel_id=1, source_target_pairs={{0,96},{1,97},{2,98},{3,99},{4,100},{5,101},{6,102},{7,103},{8,104... | collective-permute-start | bytes 442376 | tf_op jit(solution)/shard_map/ppermute | solution.py:41
where the time goes:
time: 112 us; the launch traced here: 111 us
  waiting for transfers between devices  47.9 us (43%)
  starting transfers between devices  33.5 us (30%)
  Pallas kernels  18.9 us (17%)
  local copies, waits for them, and re-layouts  6.36 us (6%)
  between operations  3.3 us (3%)
  other arithmetic  1.12 us (1%)
    ppermute x18, waiting for transfers between devices, exchange(): lax.ppermute(value, AXES, exchange_pairs(axis_core0, axis_core1, mask))  43.5 us
    ppermute x18, starting transfers between devices, exchange(): lax.ppermute(value, AXES, exchange_pairs(axis_core0, axis_core1, mask))  28.8 us
    pallas_call x5, Pallas kernels, call(): pl.pallas_call(kernel, out_shape=outs, in_specs=[smem] * len(scalars) + [...  15.7 us
    all_to_all x1, starting transfers between devices, local(): sums = lax.all_to_all(sums, ('y', 'z'), 0, 0, tiled=True)  4.12 us
    unnamed x22, local copies, waits for them, and re-layouts  3.56 us
    pallas_call x1, Pallas kernels, local(): pl.pallas_call(site_kernel, out_shape=jax.ShapeDtypeStruct((sites + 8, wi...  3.19 us
    all_to_all x1, waiting for transfers between devices, local(): sums = lax.all_to_all(sums, ('y', 'z'), 0, 0, tiled=True)  2.89 us
  transfers between devices with their start and end apart: 25, of which 14 were waited for; matrix products, arithmetic and copies ran while one was open for 3% of the time, Pallas kernels for 4%

commit v1 on v0

--- a/solution.py
+++ b/solution.py
@@ -54,13 +54,14 @@
     target_ref,
     mask_ref,
     out_ref,
+    line_ref,
     rows_ref,
     picked_ref,
     sems,
 ):
     sites = 2 * CAP
     copies = []
-    picks = lax.broadcasted_iota(I32, (sites, 8 * sites), 0)
+    picks = lax.broadcasted_iota(I32, (sites, 1), 0)
     lanes = lax.broadcasted_iota(I32, (sites, 8 * sites), 1)
     column = lax.axis_index("y") * 4 + lax.axis_index("z")
     tissues = pl.multiple_of((column // 2) * 8, 8)
@@ -98,13 +99,11 @@
     value = jnp.where(live & (masks > 0), targets, -1)
     halves = jnp.concatenate([value >> 6, value & 63], axis=1).astype(F32)
     halves = jnp.concatenate([halves, jnp.zeros_like(halves)], axis=0)
-    out_ref[sites : sites + 8, :] = halves.astype(BF16)
+    line_ref[...] = halves.astype(BF16)
 
     for copy in copies[2:]:
         copy.wait()
-    out_ref[0:sites, :] = jnp.dot(
-        onehot, rows_ref[...], preferred_element_type=F32
-    ).astype(BF16)
+    out_ref[...] = jnp.dot(onehot, rows_ref[...], preferred_element_type=F32).astype(BF16)
 
 
 def output_kernel(own_ref, one_ref, two_ref, three_ref, out_ref):
@@ -124,8 +123,12 @@
 def acceptor_tables(count_row, x, c, y, z):
     lane = lax.broadcasted_iota(I32, (1, SUB), 1)
     sub = lax.broadcasted_iota(I32, (SUB, SUB), 0)
-    m3, m2, m1 = (lane >> 4) & 3, (lane >> 2) & 3, lane & 3
-    core = c ^ (lane >> 6)
+    part = lane >> 4
+    m2, m1 = (lane >> 2) & 3, lane & 3
+    half = jnp.where(part < 6, (part * 11) >> 5, part - 6)
+    m3 = part - 3 * half
+    m3 = jnp.where(part < 6, m3 ^ (m3 >> 1), 2)
+    core = c ^ half
     shard0 = (x ^ m3) * 32 + (y ^ m1) * 4 + (z ^ m2)
     shard1 = (x ^ m2) * 32 + 16 + (y ^ m3) * 4 + (z ^ m1)
     shard = jnp.where(core == 0, shard0, shard1)
@@ -198,35 +201,47 @@
     return hit, base
 
 
-def acceptor_kernel(count_ref, lines_ref, *refs):
-    pieces = refs[:8]
-    acc_ref, offset_ref, value_ref, rank_ref, starts_ref = refs[8:]
-    width = acc_ref.shape[1]
+def table_kernel(count_ref, one_ref, two_ref, three_ref, four_ref, weights_ref, *refs):
+    offset_ref, arank_ref, value_ref, drank_ref, w_ref, astarts_ref, dstarts_ref, sem = refs
     x, c, y, z = (lax.axis_index(a) for a in AXES)
-    blocks = PIECE // SUB
-
-    rows = [
-        jnp.where(c == 0, pieces[i][PIECE : PIECE + 8, :], lines_ref[i]) for i in range(4)
-    ]
+    copy = pltpu.make_async_copy(weights_ref.at[x], w_ref, sem)
+    copy.start()
     lower = lax.broadcasted_iota(I32, (SUB, SUB), 0) <= lax.broadcasted_iota(I32, (SUB, SUB), 1)
     lower = one_hot(lower)
+    rows = [ref[...] for ref in (one_ref, two_ref, three_ref, four_ref)]
     count = 0
-    for b, row in enumerate(donor_tables(rows, x, c, y, z)):
-        starts_ref[b] = count
+    values = donor_tables(rows, x, c, y, z)
+    for b, row in enumerate(values):
+        dstarts_ref[b] = count
         active = jnp.where(row >= 0, 1.0, 0.0)
         inclusive = jnp.dot(as_rows(active), lower, preferred_element_type=F32).astype(I32)
-        rank_ref[b : b + 1, :] = jnp.where(row >= 0, inclusive[0:1, :] - 1 + count, -1)
+        drank_ref[b : b + 1, :] = jnp.where(row >= 0, inclusive[0:1, :] - 1 + count, -1)
         value_ref[b : b + 1, :] = row
         count = count + jnp.sum(active).astype(I32)
-    starts_ref[4 * blocks] = count
-
-    offset_row, ranks, starts_a = acceptor_tables(count_ref[...], x, c, y, z)
+    dstarts_ref[len(values)] = count
+    offset_row, ranks, starts = acceptor_tables(count_ref[...], x, c, y, z)
     offset_ref[...] = jnp.broadcast_to(offset_row, (8, SUB))
-    acc_ref[0:16, :] = jnp.zeros((16, width), BF16)
-    for b in range(8 * blocks):
-        i, j = b // blocks, b % blocks
-        compact(acc_ref, pieces[i][j * SUB : (j + 1) * SUB, :], ranks[b], starts_a[b])
-    acc_ref[LIVE:COLS, :] = jnp.zeros((COLS - LIVE, width), BF16)
+    for b, (rank, start) in enumerate(zip(ranks, starts)):
+        arank_ref[b : b + 1, :] = rank
+        astarts_ref[b] = start
+    copy.wait()
+
+
+def acceptor_kernel(first, starts_ref, rank_ref, *refs):
+    pieces, acc_ref = refs[:-1], refs[-1]
+    width = acc_ref.shape[1]
+    blocks = PIECE // SUB
+    if first == 0:
+        acc_ref[0:16, :] = jnp.zeros((16, width), BF16)
+    else:
+        pieces = pieces[1:]
+    for i, piece in enumerate(pieces):
+        for j in range(blocks):
+            b = (first + i) * blocks + j
+            source = piece[j * SUB : (j + 1) * SUB, :]
+            compact(acc_ref, source, rank_ref[b : b + 1, :], starts_ref[b])
+    if first:
+        acc_ref[LIVE:COLS, :] = jnp.zeros((COLS - LIVE, width), BF16)
 
 
 def head_kernel(starts_ref, acc_ref, offset_ref, value_ref, rank_ref, w_ref, *refs):
@@ -266,8 +281,10 @@
         core = (shard >> 4) & 1
         my = ((shard >> 2) & 3) ^ y
         mz = (shard & 3) ^ z
-        place = jnp.where(core == 0, mx * 16 + mz * 4 + my, my * 16 + mx * 4 + mz)
-        place = place + jnp.where(core == c, 0, 64)
+        half = jnp.where(core == c, 0, 1)
+        m3 = jnp.where(core == 0, mx, my)
+        part = jnp.where(m3 == 2, 6 + half, half * 3 + m3 - (m3 >> 1))
+        place = part * 16 + jnp.where(core == 0, mz * 4 + my, mx * 4 + mz)
         found = place == lax.broadcasted_iota(I32, (MB, SUB), 1)
         column = jnp.sum(jnp.where(found, offset_row + within, 0), axis=1, keepdims=True)
 
@@ -348,13 +365,14 @@
     part = width // 8
     vmem = pl.BlockSpec(memory_space=pltpu.VMEM)
     smem = pl.BlockSpec(memory_space=pltpu.SMEM)
-    any_space = pl.BlockSpec(memory_space=pl.ANY)
+    any_space = pl.BlockSpec(memory_space=pltpu.MemorySpace.HBM)
     sites = 2 * CAP
-    block = pl.pallas_call(
+    near = pltpu.MemorySpace.VMEM
+    block, lines = pl.pallas_call(
         site_kernel,
-        out_shape=jax.ShapeDtypeStruct((sites + 8, width), BF16),
+        out_shape=(near((sites, width), BF16), near((8, width), BF16)),
         in_specs=[smem] * 3 + [any_space] * 4,
-        out_specs=vmem,
+        out_specs=(vmem, vmem),
         scratch_shapes=[
             pltpu.VMEM((8 * sites, width), BF16),
             pltpu.VMEM((2, 8, PIECE), I32),
@@ -362,22 +380,19 @@
         ],
         name="site_rows",
     )(acceptor_pos, donor_pos, donor_count, acceptor_emb, donor_emb, target, junction_mask)
-    lines = block[sites:]
 
     block = jnp.stack([block] + [exchange(block, "y", "z", m) for m in (1, 2, 3)])
+    lines = [lines] + [exchange(lines, "x", "x", m) for m in (1, 2, 3)]
     block = jnp.stack([block] + [exchange(block, "z", "x", m) for m in (1, 2, 3)])
-    acceptors = jnp.concatenate([block[:, :, :CAP].reshape(PIECE, width), lines])
+    acceptors = block[:, :, :CAP].reshape(PIECE, width)
     donors = block[:, :, CAP:sites].reshape(PIECE, width)
-    all_lines = block[:, 0, sites:]
     acceptors = [acceptors] + [exchange(acceptors, "x", "y", m) for m in (1, 2, 3)]
     donors = [donors] + [exchange(donors, "x", "y", m) for m in (1, 2, 3)]
     others = []
     for piece in acceptors:
         others.append(swap_core(piece))
 
-    near = pltpu.MemorySpace.VMEM
-
-    def call(kernel, limit, outs, operands, scratch=(), scalars=(), specs=vmem):
+    def call(kernel, limit, outs, operands, scratch=(), scalars=(), specs=vmem, **options):
         operands = [pltpu.with_memory_space_constraint(o, near) for o in operands]
         return pl.pallas_call(
             kernel,
@@ -386,22 +401,40 @@
             out_specs=specs,
             scratch_shapes=list(scratch),
             compiler_params=pltpu.CompilerParams(vmem_limit_bytes=limit * 2**20),
+            **options,
         )(*scalars, *operands)
 
-    compacted, offsets, values, ranks, starts = call(
-        acceptor_kernel,
-        24,
-        (
-            near((ROWS_A, width), BF16),
+    offsets, aranks, values, dranks, tissue, astarts, dstarts = pl.pallas_call(
+        table_kernel,
+        out_shape=(
             near((8, SUB), I32),
+            near((24, SUB), I32),
             near((16, SUB), I32),
             near((16, SUB), I32),
+            near((width, width), BF16),
+            jax.ShapeDtypeStruct((24,), I32),
             jax.ShapeDtypeStruct((16,), I32),
         ),
-        (acceptor_count.reshape(1, 128), all_lines, *acceptors, *others),
-        specs=(vmem,) * 4 + (smem,),
-    )
-    tissue = lax.dynamic_index_in_dim(weights, lax.axis_index("x"), 0, False)
+        in_specs=[vmem] * 5 + [any_space],
+        out_specs=(vmem,) * 5 + (smem,) * 2,
+        scratch_shapes=[pltpu.SemaphoreType.DMA(())],
+        compiler_params=pltpu.CompilerParams(vmem_limit_bytes=12 * 2**20),
+        name="tables",
+    )(acceptor_count.reshape(1, 128), *lines, weights)
+
+    acc_shape = near((ROWS_A, width), BF16)
+    early = [side[m] for side in (acceptors, others) for m in (0, 1, 3)]
+    compacted = call(
+        lambda *refs: acceptor_kernel(0, *refs), 16, acc_shape, [aranks] + early, scalars=(astarts,)
+    )
+    compacted = call(
+        lambda starts_ref, rank_ref, *refs: acceptor_kernel(6, starts_ref, rank_ref, *refs),
+        16,
+        acc_shape,
+        [aranks, compacted, acceptors[2], others[2]],
+        scalars=(astarts,),
+        input_output_aliases={2: 0},
+    )
     keep, send, sums = call(
         head_kernel,
         36,
@@ -410,14 +443,14 @@
             near((4, part, width), BF16),
             near((8, SUB), F32),
         ),
-        (compacted, offsets, values, ranks, tissue, *donors),
+        (compacted, offsets, values, dranks, tissue, *donors),
         (
             pltpu.VMEM((4 * PIECE + MB + 16, width), BF16),
             pltpu.VMEM((4 * PIECE + MB + 16, SUB), I32),
             pltpu.VMEM((width, width), F32),
             pltpu.VMEM((8, SUB), F32),
         ),
-        (starts,),
+        (dstarts,),
         specs=(vmem,) * 3,
     )
 

time: 112 us -> 115 us (1.027)
  starting transfers between devices: 33.5 us -> 40.4 us
  local copies, waits for them, and re-layouts: 6.36 us -> 0.69 us
  waiting for transfers between devices: 47.9 us -> 51.9 us
    ppermute x18 -> x21, starting transfers between devices: 28.8 us -> 36.3 us  [exchange(): lax.ppermute(value, AXES, exchange_pairs(axis_core0, axis_core1, mask))]
    ppermute x18 -> x21, waiting for transfers between devices: 43.5 us -> 47.6 us  [exchange(): lax.ppermute(value, AXES, exchange_pairs(axis_core0, axis_core1, mask))]
    unnamed x22 -> x4, local copies, waits for them, and re-layouts: 3.56 us -> 0.01 us
    pallas_call x5 -> x6, Pallas kernels: 15.7 us -> 13.8 us  [call(): pl.pallas_call(kernel, out_shape=outs, in_specs=[smem] * len(scalars) + [...]
    squeeze x1 -> x0, local copies, waits for them, and re-layouts: 1.43 us -> none  [local(): tissue = lax.dynamic_index_in_dim(weights, lax.axis_index('x'), 0, False)]
    pallas_call x1 -> x2, Pallas kernels: 3.19 us -> 4.43 us  [the longest x1 2.55 us: local(): pl.pallas_call(site_kernel, out_shape=(near((sites, width), BF16), near((...]
  transfers between devices with their start and end apart: 25 -> 28, of which waited for: 14 -> 18; matrix products, arithmetic and copies ran while one was open for 3% -> 1% of each run, Pallas kernels for 4% -> 4%
where the time goes in v1:
time: 115 us
  waiting for transfers between devices  51.9 us (45%)
  starting transfers between devices  40.4 us (35%)
  Pallas kernels  18.2 us (16%)
  between operations  3.21 us (3%)
    ppermute x21, waiting for transfers between devices, exchange(): lax.ppermute(value, AXES, exchange_pairs(axis_core0, axis_core1, mask))  47.6 us
    ppermute x21, starting transfers between devices, exchange(): lax.ppermute(value, AXES, exchange_pairs(axis_core0, axis_core1, mask))  36.3 us
    pallas_call x6, Pallas kernels, call(): pl.pallas_call(kernel, out_shape=outs, in_specs=[smem] * len(scalars) + [...  13.8 us
    all_to_all x1, starting transfers between devices, local(): sums = lax.all_to_all(sums, ('y', 'z'), 0, 0, tiled=True)  3.5 us
    all_to_all x1, waiting for transfers between devices, local(): sums = lax.all_to_all(sums, ('y', 'z'), 0, 0, tiled=True)  2.82 us
    pallas_call x1, Pallas kernels, local(): pl.pallas_call(site_kernel, out_shape=(near((sites, width), BF16), near((...  2.55 us
  transfers between devices with their start and end apart: 28, of which 18 were waited for; matrix products, arithmetic and copies ran while one was open for 1% of the time, Pallas kernels for 4%

profile of v1, /device:TPU:0, one launch (start us, length us, event | category | flops | bytes accessed | tf_op | source)
XLA Modules:
  0.0 114.7 jit_solution(4147507621896986202)
XLA Ops:
  0.6 2.5 %site_rows.1 = (bf16[48,768]{1,0:T(8,128)(2,1)S(1)}, bf16[8,768]{1,0:T(8,128)(2,1)S(1)}) custom-call(s32[24]{0:T(128)} %apos_ref.1, s32[24]{0:T(128)} %dpos_ref.1, s32[16]{0:T(128)} %count_ref.1, bf16[2048,768]{1,0:T(8,128)(2,1)} %aemb_ref.1, bf16[2048,768]{1,0:T(8,128)(2,1)} %demb_ref.1, s32[64,384]{1,0:T(8,128)} %target_ref.1, s32[64,384]{1,0:T(8,128)} %mask_ref.1), custom_call_target="tpu_custom_call" | custom-call | tf_op jit(solution)/shard_map/site_rows/pallas_call | solution.py:371
  3.2 1.8 %collective-permute-start.3 = (bf16[48,768]{1,0:T(8,128)(2,1)S(1)}, bf16[48,768]{1,0:T(8,128)(2,1)S(1)}, u32[]{:S(2)}, u32[]{:S(2)}) collective-permute-start(bf16[48,768]{1,0:T(8,128)(2,1)S(1)} %get-tuple-element.23), channel_id=1, source_target_pairs={{0,4},{1,5},{2,6},{3,7},{4,0},{5,1},{6,2},{7,3},{8,12},{9,13},{10,... | collective-permute-start | bytes 221192 | tf_op jit(solution)/shard_map/ppermute | solution.py:41
  5.0 2.9 %collective-permute-start.4 = (bf16[48,768]{1,0:T(8,128)(2,1)S(1)}, bf16[48,768]{1,0:T(8,128)(2,1)S(1)}, u32[]{:S(2)}, u32[]{:S(2)}) collective-permute-start(bf16[48,768]{1,0:T(8,128)(2,1)S(1)} %get-tuple-element.23), channel_id=1, source_target_pairs={{0,8},{1,9},{2,10},{3,11},{4,12},{5,13},{6,14},{7,15},{8,0},{9,1},... | collective-permute-start | bytes 221192 | tf_op jit(solution)/shard_map/ppermute | solution.py:41
  7.9 0.1 collective-permute-start.5
  8.0 3.0 %collective-permute-done.4 = bf16[48,768]{1,0:T(8,128)(2,1)S(1)} collective-permute-done((bf16[48,768]{1,0:T(8,128)(2,1)S(1)}, bf16[48,768]{1,0:T(8,128)(2,1)S(1)}, u32[]{:S(2)}, u32[]{:S(2)}) %collective-permute-start.4) | collective-permute-done | bytes 73760 | tf_op jit(solution)/shard_map/ppermute | solution.py:41
  11.0 2.4 %collective-permute-done.5 = bf16[48,768]{1,0:T(8,128)(2,1)S(1)} collective-permute-done((bf16[48,768]{1,0:T(8,128)(2,1)S(1)}, bf16[48,768]{1,0:T(8,128)(2,1)S(1)}, u32[]{:S(2)}, u32[]{:S(2)}) %collective-permute-start.5) | collective-permute-done | bytes 73760 | tf_op jit(solution)/shard_map/ppermute | solution.py:41
  13.4 0.1 fusion
  13.5 2.0 %collective-permute-start.6 = (bf16[4,48,768]{2,1,0:T(8,128)(2,1)S(1)}, bf16[4,48,768]{2,1,0:T(8,128)(2,1)S(1)}, u32[]{:S(2)}, u32[]{:S(2)}) collective-permute-start(bf16[4,48,768]{2,1,0:T(8,128)(2,1)S(1)} %get-tuple-element.39), channel_id=1, source_target_pairs={{0,1},{1,0},{2,3},{3,2},{4,5},{5,4},{6,7},{7,6},{8,9},{9,8},{10,11... | collective-permute-start | bytes 884744 | tf_op jit(solution)/shard_map/ppermute | solution.py:41
  15.5 3.6 %collective-permute-start.7 = (bf16[4,48,768]{2,1,0:T(8,128)(2,1)S(1)}, bf16[4,48,768]{2,1,0:T(8,128)(2,1)S(1)}, u32[]{:S(2)}, u32[]{:S(2)}) collective-permute-start(bf16[4,48,768]{2,1,0:T(8,128)(2,1)S(1)} %get-tuple-element.39), channel_id=1, source_target_pairs={{0,2},{1,3},{2,0},{3,1},{4,6},{5,7},{6,4},{7,5},{8,10},{9,11},{10,... | collective-permute-start | bytes 884744 | tf_op jit(solution)/shard_map/ppermute | solution.py:41
  19.1 0.0 collective-permute-start.8
  19.1 1.2 %collective-permute-done.6 = bf16[4,48,768]{2,1,0:T(8,128)(2,1)S(1)} collective-permute-done((bf16[4,48,768]{2,1,0:T(8,128)(2,1)S(1)}, bf16[4,48,768]{2,1,0:T(8,128)(2,1)S(1)}, u32[]{:S(2)}, u32[]{:S(2)}) %collective-permute-start.6) | collective-permute-done | bytes 294944 | tf_op jit(solution)/shard_map/ppermute | solution.py:41
  20.3 6.7 %collective-permute-done.7 = bf16[4,48,768]{2,1,0:T(8,128)(2,1)S(1)} collective-permute-done((bf16[4,48,768]{2,1,0:T(8,128)(2,1)S(1)}, bf16[4,48,768]{2,1,0:T(8,128)(2,1)S(1)}, u32[]{:S(2)}, u32[]{:S(2)}) %collective-permute-start.7) | collective-permute-done | bytes 294944 | tf_op jit(solution)/shard_map/ppermute | solution.py:41
  27.0 3.1 %collective-permute-done.8 = bf16[4,48,768]{2,1,0:T(8,128)(2,1)S(1)} collective-permute-done((bf16[4,48,768]{2,1,0:T(8,128)(2,1)S(1)}, bf16[4,48,768]{2,1,0:T(8,128)(2,1)S(1)}, u32[]{:S(2)}, u32[]{:S(2)}) %collective-permute-start.8) | collective-permute-done | bytes 294944 | tf_op jit(solution)/shard_map/ppermute | solution.py:41
  30.1 0.1 pad_maximum_fusion
  30.2 0.0 copy-start.1
  30.2 0.1 fusion.1
  30.3 1.6 %collective-permute-start.9 = (bf16[384,768]{1,0:T(8,128)(2,1)S(1)}, bf16[384,768]{1,0:T(8,128)(2,1)S(1)}, u32[]{:S(2)}, u32[]{:S(2)}) collective-permute-start(bf16[384,768]{1,0:T(8,128)(2,1)S(1)} %bitcast.17), channel_id=1, source_target_pairs={{0,32},{1,33},{2,34},{3,35},{4,36},{5,37},{6,38},{7,39},{8,40},{9,... | collective-permute-start | bytes 1769480 | tf_op jit(solution)/shard_map/ppermute | solution.py:41
  31.9 2.1 %collective-permute-start.10 = (bf16[384,768]{1,0:T(8,128)(2,1)S(1)}, bf16[384,768]{1,0:T(8,128)(2,1)S(1)}, u32[]{:S(2)}, u32[]{:S(2)}) collective-permute-start(bf16[384,768]{1,0:T(8,128)(2,1)S(1)} %bitcast.18), channel_id=1, source_target_pairs={{0,96},{1,97},{2,98},{3,99},{4,100},{5,101},{6,102},{7,103},{8,104... | collective-permute-start | bytes 1769480 | tf_op jit(solution)/shard_map/ppermute | solution.py:41
  34.0 0.6 collective-permute-start.14
  34.6 0.0 collective-permute-start.11
  34.6 5.7 %collective-permute-done.9.refs_3_ = bf16[384,768]{1,0:T(8,128)(2,1)S(1)} collective-permute-done((bf16[384,768]{1,0:T(8,128)(2,1)S(1)}, bf16[384,768]{1,0:T(8,128)(2,1)S(1)}, u32[]{:S(2)}, u32[]{:S(2)}) %collective-permute-start.9) | collective-permute-done | bytes 589856 | tf_op jit(solution)/shard_map/ppermute | solution.py:41
  40.3 0.0 collective-permute-start.12
  40.3 1.5 %collective-permute-start = (bf16[8,768]{1,0:T(8,128)(2,1)S(1)}, bf16[8,768]{1,0:T(8,128)(2,1)S(1)}, u32[]{:S(2)}, u32[]{:S(2)}) collective-permute-start(bf16[8,768]{1,0:T(8,128)(2,1)S(1)} %get-tuple-element.19.one_ref), channel_id=1, source_target_pairs={{0,32},{1,33},{2,34},{3,35},{4,36},{5,37},{6,38},{7,39},{8,40},{9,... | collective-permute-start | bytes 36872 | tf_op jit(solution)/shard_map/ppermute | solution.py:41
  41.8 5.1 %collective-permute-done.two_ref = bf16[8,768]{1,0:T(8,128)(2,1)S(1)} collective-permute-done((bf16[8,768]{1,0:T(8,128)(2,1)S(1)}, bf16[8,768]{1,0:T(8,128)(2,1)S(1)}, u32[]{:S(2)}, u32[]{:S(2)}) %collective-permute-start) | collective-permute-done | bytes 12320 | tf_op jit(solution)/shard_map/ppermute | solution.py:41
  46.9 3.0 %collective-permute-start.1 = (bf16[8,768]{1,0:T(8,128)(2,1)S(1)}, bf16[8,768]{1,0:T(8,128)(2,1)S(1)}, u32[]{:S(2)}, u32[]{:S(2)}) collective-permute-start(bf16[8,768]{1,0:T(8,128)(2,1)S(1)} %get-tuple-element.19.one_ref), channel_id=1, source_target_pairs={{0,64},{1,65},{2,66},{3,67},{4,68},{5,69},{6,70},{7,71},{8,72},{9,... | collective-permute-start | bytes 36872 | tf_op jit(solution)/shard_map/ppermute | solution.py:41
  49.9 2.2 %collective-permute-done.1.three_ref = bf16[8,768]{1,0:T(8,128)(2,1)S(1)} collective-permute-done((bf16[8,768]{1,0:T(8,128)(2,1)S(1)}, bf16[8,768]{1,0:T(8,128)(2,1)S(1)}, u32[]{:S(2)}, u32[]{:S(2)}) %collective-permute-start.1) | collective-permute-done | bytes 12320 | tf_op jit(solution)/shard_map/ppermute | solution.py:41
  52.1 2.9 %collective-permute-start.2 = (bf16[8,768]{1,0:T(8,128)(2,1)S(1)}, bf16[8,768]{1,0:T(8,128)(2,1)S(1)}, u32[]{:S(2)}, u32[]{:S(2)}) collective-permute-start(bf16[8,768]{1,0:T(8,128)(2,1)S(1)} %get-tuple-element.19.one_ref), channel_id=1, source_target_pairs={{0,96},{1,97},{2,98},{3,99},{4,100},{5,101},{6,102},{7,103},{8,104... | collective-permute-start | bytes 36872 | tf_op jit(solution)/shard_map/ppermute | solution.py:41
  55.0 0.0 collective-permute-done.10.refs_4_
  55.0 2.0 %collective-permute-done.2.four_ref = bf16[8,768]{1,0:T(8,128)(2,1)S(1)} collective-permute-done((bf16[8,768]{1,0:T(8,128)(2,1)S(1)}, bf16[8,768]{1,0:T(8,128)(2,1)S(1)}, u32[]{:S(2)}, u32[]{:S(2)}) %collective-permute-start.2) | collective-permute-done | bytes 12320 | tf_op jit(solution)/shard_map/ppermute | solution.py:41
  57.0 0.3 collective-permute-start.16
  57.3 0.0 collective-permute-done.14.refs_1_
  57.3 0.0 collective-permute-start.15
  57.3 0.0 collective-permute-done.11.refs_5_
  57.3 4.2 %collective-permute-start.17 = (bf16[384,768]{1,0:T(8,128)(2,1)S(1)}, bf16[384,768]{1,0:T(8,128)(2,1)S(1)}, u32[]{:S(2)}, u32[]{:S(2)}) collective-permute-start(bf16[384,768]{1,0:T(8,128)(2,1)S(1)} %bitcast.14), channel_id=1, source_target_pairs={{0,64},{1,65},{2,66},{3,67},{4,68},{5,69},{6,70},{7,71},{8,72},{9,... | collective-permute-start | bytes 1769480 | tf_op jit(solution)/shard_map/ppermute | solution.py:41
  61.5 0.4 collective-permute-start.18
  61.8 1.9 %tables.1 = (s32[8,128]{1,0:T(8,128)S(1)}, s32[24,128]{1,0:T(8,128)S(1)}, s32[16,128]{1,0:T(8,128)S(1)}, s32[16,128]{1,0:T(8,128)S(1)}, bf16[768,768]{1,0:T(8,12...) custom-call(s32[1,128]{1,0:T(1,128)S(1)} %bitcast.23, bf16[8,768]{1,0:T(8,128)(2,1)S(1)} %get-tuple-element.19.one_ref, ...), custom_call_target="tpu_custom_call" | custom-call | tf_op jit(solution)/shard_map/tables/pallas_call | solution.py:407
  63.7 0.0 collective-permute-done.13.refs_7_
  63.7 1.8 %shard_map.104.refs_0_ = bf16[1744,768]{1,0:T(8,128)(2,1)S(1)} custom-call(s32[24]{0:T(128)S(1)} %get-tuple-element.21.refs_0_.starts_ref, s32[24,128]{1,0:T(8,128)S(1)} %get-tuple-element.22.refs_1_.rank_ref, bf16[384,768]{1,0:T(8,128)(2,1)S(1)} %bitcast.21, bf16[384,768]{1,0:T(8,128)(2,1)S(1)} %collective-permute-done.9.refs_3_, ...), custom_call_target="tpu_custom_call" | custom-call | tf_op jit(solution)/shard_map/pallas_call | solution.py:397
  65.5 0.0 collective-permute-done.15.refs_2_
  65.5 1.0 shard_map.105.acc_ref
  66.6 0.4 collective-permute-done.16.refs_1_
  66.9 8.7 %collective-permute-done.17.refs_2_ = bf16[384,768]{1,0:T(8,128)(2,1)S(1)} collective-permute-done((bf16[384,768]{1,0:T(8,128)(2,1)S(1)}, bf16[384,768]{1,0:T(8,128)(2,1)S(1)}, u32[]{:S(2)}, u32[]{:S(2)}) %collective-permute-start.17) | collective-permute-done | bytes 589856 | tf_op jit(solution)/shard_map/ppermute | solution.py:41
  75.7 3.2 %collective-permute-done.18.refs_3_ = bf16[384,768]{1,0:T(8,128)(2,1)S(1)} collective-permute-done((bf16[384,768]{1,0:T(8,128)(2,1)S(1)}, bf16[384,768]{1,0:T(8,128)(2,1)S(1)}, u32[]{:S(2)}, u32[]{:S(2)}) %collective-permute-start.18) | collective-permute-done | bytes 589856 | tf_op jit(solution)/shard_map/ppermute | solution.py:41
  78.9 9.0 %shard_map.106 = (f32[4,96,768]{2,1,0:T(8,128)S(1)}, bf16[4,96,768]{2,1,0:T(8,128)(2,1)S(1)}, f32[8,128]{1,0:T(8,128)S(1)}) custom-call(s32[16]{0:T(128)S(1)} %get-tuple-element.20.starts_ref, bf16[1744,768]{1,0:T(8,128)(2,1)S(1)} %shard_map.105.acc_ref, s32[8,128]{1,0:T(8,128)S(1)} %get-tuple-element.24.offset_ref, ...), custom_call_target="tpu_custom_call" | custom-call | tf_op jit(solution)/shard_map/pallas_call | solution.py:397
  87.9 0.1 collective-permute-start.19
  88.0 0.5 collective-permute-start.20
  88.5 1.5 %collective-permute-done.20.other_ref = f32[8,128]{1,0:T(8,128)S(1)} collective-permute-done((f32[8,128]{1,0:T(8,128)S(1)}, f32[8,128]{1,0:T(8,128)S(1)}, u32[]{:S(2)}, u32[]{:S(2)}) %collective-permute-start.20) | collective-permute-done | bytes 4128 | tf_op jit(solution)/shard_map/ppermute | solution.py:45
  90.0 0.0 collective-permute-done.19.received_ref
  90.0 0.1 shard_map.107
  90.1 0.1 collective-permute-start.21
  90.2 1.8 %collective-permute-start.22 = (f32[8,128]{1,0:T(8,128)S(1)}, f32[8,128]{1,0:T(8,128)S(1)}, u32[]{:S(2)}, u32[]{:S(2)}) collective-permute-start(f32[8,128]{1,0:T(8,128)S(1)} %get-tuple-element.31.own_ref), channel_id=1, source_target_pairs={{0,64},{1,65},{2,66},{3,67},{4,68},{5,69},{6,70},{7,71},{8,72},{9,... | collective-permute-start | bytes 12296 | tf_op jit(solution)/shard_map/ppermute | solution.py:41
  92.0 2.9 %collective-permute-start.23 = (f32[8,128]{1,0:T(8,128)S(1)}, f32[8,128]{1,0:T(8,128)S(1)}, u32[]{:S(2)}, u32[]{:S(2)}) collective-permute-start(f32[8,128]{1,0:T(8,128)S(1)} %get-tuple-element.31.own_ref), channel_id=1, source_target_pairs={{0,96},{1,97},{2,98},{3,99},{4,100},{5,101},{6,102},{7,103},{8,104... | collective-permute-start | bytes 12296 | tf_op jit(solution)/shard_map/ppermute | solution.py:41
  94.9 0.5 collective-permute-done.22.two_ref
  95.4 1.4 %collective-permute-done.23.three_ref = f32[8,128]{1,0:T(8,128)S(1)} collective-permute-done((f32[8,128]{1,0:T(8,128)S(1)}, f32[8,128]{1,0:T(8,128)S(1)}, u32[]{:S(2)}, u32[]{:S(2)}) %collective-permute-start.23) | collective-permute-done | bytes 4128 | tf_op jit(solution)/shard_map/ppermute | solution.py:41
  96.8 0.6 shard_map.108
  97.4 3.5 %all-to-all-start = ((f32[16,8,128]{2,1,0:T(8,128)}), f32[16,8,128]{2,1,0:T(8,128)S(1)}, u32[]{:S(2)}, u32[]{:S(2)}) async-start(f32[16,8,128]{2,1,0:T(8,128)} %shard_map.108), calls=%async_computation | async-start | bytes 131072 | tf_op jit(solution)/shard_map/all_to_all | solution.py:473
  100.9 0.6 collective-permute-start.24
  101.5 3.8 %collective-permute-start.25 = (bf16[96,768]{1,0:T(8,128)(2,1)S(1)}, bf16[96,768]{1,0:T(8,128)(2,1)S(1)}, u32[]{:S(2)}, u32[]{:S(2)}) collective-permute-start(bf16[96,768]{1,0:T(8,128)(2,1)S(1)} %get-tuple-element.34), channel_id=1, source_target_pairs={{0,64},{1,65},{2,66},{3,67},{4,68},{5,69},{6,70},{7,71},{8,72},{9,... | collective-permute-start | bytes 442376 | tf_op jit(solution)/shard_map/ppermute | solution.py:41
  105.4 0.4 collective-permute-start.26
  105.7 2.8 %all-to-all-done = f32[16,8,128]{2,1,0:T(8,128)S(1)} async-done(((f32[16,8,128]{2,1,0:T(8,128)}), f32[16,8,128]{2,1,0:T(8,128)S(1)}, u32[]{:S(2)}, u32[]{:S(2)}) %all-to-all-start) | async-done | bytes 65568 | tf_op jit(solution)/shard_map/all_to_all | solution.py:473
  108.6 0.6 fusion.2
  110.5 0.3 collective-permute-done.25.two_ref
  110.8 1.5 %collective-permute-done.26.three_ref = bf16[96,768]{1,0:T(8,128)(2,1)S(1)} collective-permute-done((bf16[96,768]{1,0:T(8,128)(2,1)S(1)}, bf16[96,768]{1,0:T(8,128)(2,1)S(1)}, u32[]{:S(2)}, u32[]{:S(2)}) %collective-permute-start.26) | collective-permute-done | bytes 147488 | tf_op jit(solution)/shard_map/ppermute | solution.py:41
  112.3 1.3 %shard_map.109 = f32[96,4,768]{2,1,0:T(4,128)} custom-call(bf16[96,768]{1,0:T(8,128)(2,1)S(1)} %get-tuple-element.32.own_ref, bf16[96,768]{1,0:T(8,128)(2,1)S(1)} %collective-permute-done.24.one_ref, bf16[96,768]{1,0:T(8,128)(2,1)S(1)} %collective-permute-done.25.two_ref, bf16[96,768]{1,0:T(8,128)(2,1)S(1)} %collective-permute-done.26.three_ref), custom_call_target="tpu_custom_call" | custom-call | tf_op jit(solution)/shard_map/pallas_call | solution.py:397
  (9 shorter events, 0.1 us)
Async XLA Ops:
  3.2 4.8 %collective-permute-start.3 = (bf16[48,768]{1,0:T(8,128)(2,1)S(1)}, bf16[48,768]{1,0:T(8,128)(2,1)S(1)}, u32[]{:S(2)}, u32[]{:S(2)}) collective-permute-start(bf16[48,768]{1,0:T(8,128)(2,1)S(1)} %get-tuple-element.23), channel_id=1, source_target_pairs={{0,4},{1,5},{2,6},{3,7},{4,0},{5,1},{6,2},{7,3},{8,12},{9,13},{10,... | collective-permute-start | bytes 221192 | tf_op jit(solution)/shard_map/ppermute | solution.py:41
  5.0 6.0 %collective-permute-start.4 = (bf16[48,768]{1,0:T(8,128)(2,1)S(1)}, bf16[48,768]{1,0:T(8,128)(2,1)S(1)}, u32[]{:S(2)}, u32[]{:S(2)}) collective-permute-start(bf16[48,768]{1,0:T(8,128)(2,1)S(1)} %get-tuple-element.23), channel_id=1, source_target_pairs={{0,8},{1,9},{2,10},{3,11},{4,12},{5,13},{6,14},{7,15},{8,0},{9,1},... | collective-permute-start | bytes 221192 | tf_op jit(solution)/shard_map/ppermute | solution.py:41
  7.9 5.6 %collective-permute-start.5 = (bf16[48,768]{1,0:T(8,128)(2,1)S(1)}, bf16[48,768]{1,0:T(8,128)(2,1)S(1)}, u32[]{:S(2)}, u32[]{:S(2)}) collective-permute-start(bf16[48,768]{1,0:T(8,128)(2,1)S(1)} %get-tuple-element.23), channel_id=1, source_target_pairs={{0,12},{1,13},{2,14},{3,15},{4,8},{5,9},{6,10},{7,11},{8,4},{9,5},... | collective-permute-start | bytes 221192 | tf_op jit(solution)/shard_map/ppermute | solution.py:41
  13.5 6.8 %collective-permute-start.6 = (bf16[4,48,768]{2,1,0:T(8,128)(2,1)S(1)}, bf16[4,48,768]{2,1,0:T(8,128)(2,1)S(1)}, u32[]{:S(2)}, u32[]{:S(2)}) collective-permute-start(bf16[4,48,768]{2,1,0:T(8,128)(2,1)S(1)} %get-tuple-element.39), channel_id=1, source_target_pairs={{0,1},{1,0},{2,3},{3,2},{4,5},{5,4},{6,7},{7,6},{8,9},{9,8},{10,11... | collective-permute-start | bytes 884744 | tf_op jit(solution)/shard_map/ppermute | solution.py:41
  15.5 11.5 %collective-permute-start.7 = (bf16[4,48,768]{2,1,0:T(8,128)(2,1)S(1)}, bf16[4,48,768]{2,1,0:T(8,128)(2,1)S(1)}, u32[]{:S(2)}, u32[]{:S(2)}) collective-permute-start(bf16[4,48,768]{2,1,0:T(8,128)(2,1)S(1)} %get-tuple-element.39), channel_id=1, source_target_pairs={{0,2},{1,3},{2,0},{3,1},{4,6},{5,7},{6,4},{7,5},{8,10},{9,11},{10,... | collective-permute-start | bytes 884744 | tf_op jit(solution)/shard_map/ppermute | solution.py:41
  19.1 11.0 %collective-permute-start.8 = (bf16[4,48,768]{2,1,0:T(8,128)(2,1)S(1)}, bf16[4,48,768]{2,1,0:T(8,128)(2,1)S(1)}, u32[]{:S(2)}, u32[]{:S(2)}) collective-permute-start(bf16[4,48,768]{2,1,0:T(8,128)(2,1)S(1)} %get-tuple-element.39), channel_id=1, source_target_pairs={{0,3},{1,2},{2,1},{3,0},{4,7},{5,6},{6,5},{7,4},{8,11},{9,10},{10,... | collective-permute-start | bytes 884744 | tf_op jit(solution)/shard_map/ppermute | solution.py:41
  30.1 31.8 %copy-start = (bf16[4,768,768]{2,1,0:T(8,128)(2,1)S(1)}, bf16[4,768,768]{2,1,0:T(8,128)(2,1)}, u32[]{:S(2)}) copy-start(bf16[4,768,768]{2,1,0:T(8,128)(2,1)} %weights_ref.1) | copy-start | bytes 14155780
  30.2 31.6 %copy-start.1 = (s32[128]{0:T(128)S(1)}, s32[128]{0:T(128)}, u32[]{:S(2)}) copy-start(s32[128]{0:T(128)} %param.14) | copy-start | bytes 1540
  30.3 10.0 %collective-permute-start.9 = (bf16[384,768]{1,0:T(8,128)(2,1)S(1)}, bf16[384,768]{1,0:T(8,128)(2,1)S(1)}, u32[]{:S(2)}, u32[]{:S(2)}) collective-permute-start(bf16[384,768]{1,0:T(8,128)(2,1)S(1)} %bitcast.17), channel_id=1, source_target_pairs={{0,32},{1,33},{2,34},{3,35},{4,36},{5,37},{6,38},{7,39},{8,40},{9,... | collective-permute-start | bytes 1769480 | tf_op jit(solution)/shard_map/ppermute | solution.py:41
  31.9 23.1 %collective-permute-start.10 = (bf16[384,768]{1,0:T(8,128)(2,1)S(1)}, bf16[384,768]{1,0:T(8,128)(2,1)S(1)}, u32[]{:S(2)}, u32[]{:S(2)}) collective-permute-start(bf16[384,768]{1,0:T(8,128)(2,1)S(1)} %bitcast.18), channel_id=1, source_target_pairs={{0,96},{1,97},{2,98},{3,99},{4,100},{5,101},{6,102},{7,103},{8,104... | collective-permute-start | bytes 1769480 | tf_op jit(solution)/shard_map/ppermute | solution.py:41
  34.0 23.3 %collective-permute-start.14 = (bf16[384,768]{1,0:T(8,128)(2,1)S(1)}, bf16[384,768]{1,0:T(8,128)(2,1)S(1)}, u32[]{:S(2)}, u32[]{:S(2)}) collective-permute-start(bf16[384,768]{1,0:T(8,128)(2,1)S(1)} %bitcast.19), channel_id=1, source_target_pairs={{0,64},{1,65},{2,66},{3,67},{4,68},{5,69},{6,70},{7,71},{8,72},{9,... | collective-permute-start | bytes 1769480 | tf_op jit(solution)/shard_map/ppermute | solution.py:41
  34.6 22.7 %collective-permute-start.11 = (bf16[384,768]{1,0:T(8,128)(2,1)S(1)}, bf16[384,768]{1,0:T(8,128)(2,1)S(1)}, u32[]{:S(2)}, u32[]{:S(2)}) collective-permute-start(bf16[384,768]{1,0:T(8,128)(2,1)S(1)} %bitcast.20), channel_id=1, source_target_pairs={{0,16},{16,0},{1,17},{17,1},{2,18},{18,2},{3,19},{19,3},{4,20},{20... | collective-permute-start | bytes 1769480 | tf_op jit(solution)/shard_map/ppermute | solution.py:45
  40.3 21.2 %collective-permute-start.12 = (bf16[384,768]{1,0:T(8,128)(2,1)S(1)}, bf16[384,768]{1,0:T(8,128)(2,1)S(1)}, u32[]{:S(2)}, u32[]{:S(2)}) collective-permute-start(bf16[384,768]{1,0:T(8,128)(2,1)S(1)} %collective-permute-done.9.refs_3_), channel_id=1, source_target_pairs={{0,16},{16,0},{1,17},{17,1},{2,18},{18,2},{3,19},{19,3},{4,20},{20... | collective-permute-start | bytes 1769480 | tf_op jit(solution)/shard_map/ppermute | solution.py:45
  40.3 6.6 %collective-permute-start = (bf16[8,768]{1,0:T(8,128)(2,1)S(1)}, bf16[8,768]{1,0:T(8,128)(2,1)S(1)}, u32[]{:S(2)}, u32[]{:S(2)}) collective-permute-start(bf16[8,768]{1,0:T(8,128)(2,1)S(1)} %get-tuple-element.19.one_ref), channel_id=1, source_target_pairs={{0,32},{1,33},{2,34},{3,35},{4,36},{5,37},{6,38},{7,39},{8,40},{9,... | collective-permute-start | bytes 36872 | tf_op jit(solution)/shard_map/ppermute | solution.py:41
  46.9 5.2 %collective-permute-start.1 = (bf16[8,768]{1,0:T(8,128)(2,1)S(1)}, bf16[8,768]{1,0:T(8,128)(2,1)S(1)}, u32[]{:S(2)}, u32[]{:S(2)}) collective-permute-start(bf16[8,768]{1,0:T(8,128)(2,1)S(1)} %get-tuple-element.19.one_ref), channel_id=1, source_target_pairs={{0,64},{1,65},{2,66},{3,67},{4,68},{5,69},{6,70},{7,71},{8,72},{9,... | collective-permute-start | bytes 36872 | tf_op jit(solution)/shard_map/ppermute | solution.py:41
  52.1 4.9 %collective-permute-start.2 = (bf16[8,768]{1,0:T(8,128)(2,1)S(1)}, bf16[8,768]{1,0:T(8,128)(2,1)S(1)}, u32[]{:S(2)}, u32[]{:S(2)}) collective-permute-start(bf16[8,768]{1,0:T(8,128)(2,1)S(1)} %get-tuple-element.19.one_ref), channel_id=1, source_target_pairs={{0,96},{1,97},{2,98},{3,99},{4,100},{5,101},{6,102},{7,103},{8,104... | collective-permute-start | bytes 36872 | tf_op jit(solution)/shard_map/ppermute | solution.py:41
  55.0 8.7 %collective-permute-start.13 = (bf16[384,768]{1,0:T(8,128)(2,1)S(1)}, bf16[384,768]{1,0:T(8,128)(2,1)S(1)}, u32[]{:S(2)}, u32[]{:S(2)}) collective-permute-start(bf16[384,768]{1,0:T(8,128)(2,1)S(1)} %collective-permute-done.10.refs_4_), channel_id=1, source_target_pairs={{0,16},{16,0},{1,17},{17,1},{2,18},{18,2},{3,19},{19,3},{4,20},{20... | collective-permute-start | bytes 1769480 | tf_op jit(solution)/shard_map/ppermute | solution.py:45
  57.0 9.9 %collective-permute-start.16 = (bf16[384,768]{1,0:T(8,128)(2,1)S(1)}, bf16[384,768]{1,0:T(8,128)(2,1)S(1)}, u32[]{:S(2)}, u32[]{:S(2)}) collective-permute-start(bf16[384,768]{1,0:T(8,128)(2,1)S(1)} %bitcast.13), channel_id=1, source_target_pairs={{0,32},{1,33},{2,34},{3,35},{4,36},{5,37},{6,38},{7,39},{8,40},{9,... | collective-permute-start | bytes 1769480 | tf_op jit(solution)/shard_map/ppermute | solution.py:41
  57.3 8.2 %collective-permute-start.15 = (bf16[384,768]{1,0:T(8,128)(2,1)S(1)}, bf16[384,768]{1,0:T(8,128)(2,1)S(1)}, u32[]{:S(2)}, u32[]{:S(2)}) collective-permute-start(bf16[384,768]{1,0:T(8,128)(2,1)S(1)} %collective-permute-done.14.refs_1_), channel_id=1, source_target_pairs={{0,16},{16,0},{1,17},{17,1},{2,18},{18,2},{3,19},{19,3},{4,20},{20... | collective-permute-start | bytes 1769480 | tf_op jit(solution)/shard_map/ppermute | solution.py:45
  57.3 18.3 %collective-permute-start.17 = (bf16[384,768]{1,0:T(8,128)(2,1)S(1)}, bf16[384,768]{1,0:T(8,128)(2,1)S(1)}, u32[]{:S(2)}, u32[]{:S(2)}) collective-permute-start(bf16[384,768]{1,0:T(8,128)(2,1)S(1)} %bitcast.14), channel_id=1, source_target_pairs={{0,64},{1,65},{2,66},{3,67},{4,68},{5,69},{6,70},{7,71},{8,72},{9,... | collective-permute-start | bytes 1769480 | tf_op jit(solution)/shard_map/ppermute | solution.py:41
  61.5 17.4 %collective-permute-start.18 = (bf16[384,768]{1,0:T(8,128)(2,1)S(1)}, bf16[384,768]{1,0:T(8,128)(2,1)S(1)}, u32[]{:S(2)}, u32[]{:S(2)}) collective-permute-start(bf16[384,768]{1,0:T(8,128)(2,1)S(1)} %bitcast.15), channel_id=1, source_target_pairs={{0,96},{1,97},{2,98},{3,99},{4,100},{5,101},{6,102},{7,103},{8,104... | collective-permute-start | bytes 1769480 | tf_op jit(solution)/shard_map/ppermute | solution.py:41
  87.9 2.1 %collective-permute-start.19 = (bf16[4,96,768]{2,1,0:T(8,128)(2,1)S(1)}, bf16[4,96,768]{2,1,0:T(8,128)(2,1)S(1)}, u32[]{:S(2)}, u32[]{:S(2)}) collective-permute-start(bf16[4,96,768]{2,1,0:T(8,128)(2,1)S(1)} %get-tuple-element.29), channel_id=1, source_target_pairs={{0,16},{16,0},{1,17},{17,1},{2,18},{18,2},{3,19},{19,3},{4,20},{20... | collective-permute-start | bytes 1769480 | tf_op jit(solution)/shard_map/ppermute | solution.py:45
  88.0 2.0 %collective-permute-start.20 = (f32[8,128]{1,0:T(8,128)S(1)}, f32[8,128]{1,0:T(8,128)S(1)}, u32[]{:S(2)}, u32[]{:S(2)}) collective-permute-start(f32[8,128]{1,0:T(8,128)S(1)} %get-tuple-element.30.sums_ref), channel_id=1, source_target_pairs={{0,16},{16,0},{1,17},{17,1},{2,18},{18,2},{3,19},{19,3},{4,20},{20... | collective-permute-start | bytes 12296 | tf_op jit(solution)/shard_map/ppermute | solution.py:45
  90.1 4.8 %collective-permute-start.21 = (f32[8,128]{1,0:T(8,128)S(1)}, f32[8,128]{1,0:T(8,128)S(1)}, u32[]{:S(2)}, u32[]{:S(2)}) collective-permute-start(f32[8,128]{1,0:T(8,128)S(1)} %get-tuple-element.31.own_ref), channel_id=1, source_target_pairs={{0,32},{1,33},{2,34},{3,35},{4,36},{5,37},{6,38},{7,39},{8,40},{9,... | collective-permute-start | bytes 12296 | tf_op jit(solution)/shard_map/ppermute | solution.py:41
  90.2 5.2 %collective-permute-start.22 = (f32[8,128]{1,0:T(8,128)S(1)}, f32[8,128]{1,0:T(8,128)S(1)}, u32[]{:S(2)}, u32[]{:S(2)}) collective-permute-start(f32[8,128]{1,0:T(8,128)S(1)} %get-tuple-element.31.own_ref), channel_id=1, source_target_pairs={{0,64},{1,65},{2,66},{3,67},{4,68},{5,69},{6,70},{7,71},{8,72},{9,... | collective-permute-start | bytes 12296 | tf_op jit(solution)/shard_map/ppermute | solution.py:41
  92.0 4.8 %collective-permute-start.23 = (f32[8,128]{1,0:T(8,128)S(1)}, f32[8,128]{1,0:T(8,128)S(1)}, u32[]{:S(2)}, u32[]{:S(2)}) collective-permute-start(f32[8,128]{1,0:T(8,128)S(1)} %get-tuple-element.31.own_ref), channel_id=1, source_target_pairs={{0,96},{1,97},{2,98},{3,99},{4,100},{5,101},{6,102},{7,103},{8,104... | collective-permute-start | bytes 12296 | tf_op jit(solution)/shard_map/ppermute | solution.py:41
  97.4 11.1 %all-to-all-start = ((f32[16,8,128]{2,1,0:T(8,128)}), f32[16,8,128]{2,1,0:T(8,128)S(1)}, u32[]{:S(2)}, u32[]{:S(2)}) async-start(f32[16,8,128]{2,1,0:T(8,128)} %shard_map.108), calls=%async_computation | async-start | bytes 131072 | tf_op jit(solution)/shard_map/all_to_all | solution.py:473
  100.9 9.5 %collective-permute-start.24 = (bf16[96,768]{1,0:T(8,128)(2,1)S(1)}, bf16[96,768]{1,0:T(8,128)(2,1)S(1)}, u32[]{:S(2)}, u32[]{:S(2)}) collective-permute-start(bf16[96,768]{1,0:T(8,128)(2,1)S(1)} %get-tuple-element.33), channel_id=1, source_target_pairs={{0,32},{1,33},{2,34},{3,35},{4,36},{5,37},{6,38},{7,39},{8,40},{9,... | collective-permute-start | bytes 442376 | tf_op jit(solution)/shard_map/ppermute | solution.py:41
  101.5 9.3 %collective-permute-start.25 = (bf16[96,768]{1,0:T(8,128)(2,1)S(1)}, bf16[96,768]{1,0:T(8,128)(2,1)S(1)}, u32[]{:S(2)}, u32[]{:S(2)}) collective-permute-start(bf16[96,768]{1,0:T(8,128)(2,1)S(1)} %get-tuple-element.34), channel_id=1, source_target_pairs={{0,64},{1,65},{2,66},{3,67},{4,68},{5,69},{6,70},{7,71},{8,72},{9,... | collective-permute-start | bytes 442376 | tf_op jit(solution)/shard_map/ppermute | solution.py:41
  105.4 7.0 %collective-permute-start.26 = (bf16[96,768]{1,0:T(8,128)(2,1)S(1)}, bf16[96,768]{1,0:T(8,128)(2,1)S(1)}, u32[]{:S(2)}, u32[]{:S(2)}) collective-permute-start(bf16[96,768]{1,0:T(8,128)(2,1)S(1)} %get-tuple-element.35), channel_id=1, source_target_pairs={{0,96},{1,97},{2,98},{3,99},{4,100},{5,101},{6,102},{7,103},{8,104... | collective-permute-start | bytes 442376 | tf_op jit(solution)/shard_map/ppermute | solution.py:41
